TPU v7x, 32 devices: a whole 2x2x4 slice. The times are simulated.
32 devices in a mesh: ep: 32 (over z, y, x, core).
Axes of the slice: x: 2, y: 2, z: 4, core: 2. Of those that a mesh axis runs over, the one named last changes fastest.
Arguments:
- tokens: bfloat16 [128, 64, 768], P('ep')
- loss_weight: bfloat16 [128, 64, 768], P('ep')
- w_gate: bfloat16 [768, 32], replicated
- w_in: bfloat16 [32, 768, 3072], P('ep')
- w_out: bfloat16 [32, 3072, 768], P('ep')
- first_expert: int32 [128, 64], P('ep')
- second_expert: int32 [128, 64], P('ep')
- keep_second: int32 [128, 64], P('ep')
Outputs:
- output 1: float32 [], replicated
- output 2: bfloat16 [128, 64, 768], P('ep')
- output 3: bfloat16 [32, 768, 3072], P('ep')
- output 4: bfloat16 [32, 3072, 768], P('ep')
- output 5: float32 [768, 32], replicated
All inputs are finite; a program needn't handle non-finite values.
Results may differ from a plain program's by a relative error of at most 0.00948372.
Values are sent between devices in bfloat16 or wider.
A program may use at most 1 GiB of HBM per device.

v0:
```python
import jax
import jax.numpy as jnp
from jax import lax
from jax.sharding import PartitionSpec as P

ALPHA = 0.01


def gelu_bf16(pre_act):
    return jax.nn.gelu(pre_act, approximate=True).astype(jnp.bfloat16)


def route_masks(first_ids, second_ids, keep_ids, experts, cap_rows):
    seq_len = first_ids.shape[1]
    expert_ids = jnp.arange(experts, dtype=jnp.int32)
    first_hot = (first_ids[..., None] == expert_ids).astype(jnp.bfloat16)
    second_hot = (second_ids[..., None] == expert_ids).astype(jnp.bfloat16)
    second_kept = second_hot * keep_ids.astype(jnp.bfloat16)[..., None]
    seq_ids = jnp.arange(seq_len, dtype=jnp.int32)
    earlier = (seq_ids[:, None] > seq_ids[None, :]).astype(jnp.bfloat16)
    before_first = jnp.einsum('st,gte->gse', earlier, first_hot, preferred_element_type=jnp.float32)
    before_second = jnp.einsum('st,gte->gse', earlier, second_kept, preferred_element_type=jnp.float32)
    first_count = jnp.sum(first_hot, axis=1, dtype=jnp.float32)
    pos_first = jnp.sum(before_first * first_hot, axis=-1)
    pos_second = jnp.sum((before_second + first_count[:, None, :]) * second_hot, axis=-1)
    slot_ids = jnp.arange(cap_rows, dtype=jnp.float32)
    disp_first = first_hot[..., None] * (pos_first[..., None, None] == slot_ids).astype(jnp.bfloat16)
    disp_second = second_kept[..., None] * (pos_second[..., None, None] == slot_ids).astype(jnp.bfloat16)
    return first_hot, second_hot, first_count, disp_first, disp_second


def solution(mesh):
    ep_size = mesh.shape['ep']

    def layer_body(x_loc, r_loc, w_gate, w_in_loc, w_out_loc, first_ids, second_ids, keep_ids):
        local_groups, seq_len, hidden = x_loc.shape
        experts = w_gate.shape[1]
        cap_rows = 2 * seq_len // experts
        tokens_all = local_groups * ep_size * seq_len
        numel = tokens_all * hidden
        first_hot, second_hot, first_count, disp_first, disp_second = route_masks(first_ids, second_ids, keep_ids, experts, cap_rows)
        logits = jnp.einsum('gsh,he->gse', x_loc, w_gate, preferred_element_type=jnp.float32)
        router_prob = jax.nn.softmax(logits, axis=-1)
        gate_first = jnp.sum(router_prob * first_hot, axis=-1)
        gate_second = jnp.sum(router_prob * second_hot, axis=-1)
        gate_sum = gate_first + gate_second
        norm_first = (gate_first / gate_sum).astype(jnp.bfloat16)
        norm_second = (gate_second / gate_sum).astype(jnp.bfloat16)
        dispatch = disp_first + disp_second
        combine = disp_first * norm_first[..., None, None] + disp_second * norm_second[..., None, None]
        send_x = jnp.einsum('gsec,gsh->egch', dispatch, x_loc, preferred_element_type=jnp.float32).astype(jnp.bfloat16)
        expert_x = lax.all_to_all(send_x, 'ep', 0, 1, tiled=True)
        pre_act = jnp.einsum('egch,ehf->egcf', expert_x, w_in_loc, preferred_element_type=jnp.float32)
        act_bf, act_pull = jax.vjp(gelu_bf16, pre_act)
        expert_y = jnp.einsum('egcf,efh->egch', act_bf, w_out_loc, preferred_element_type=jnp.float32).astype(jnp.bfloat16)
        back_y = lax.all_to_all(expert_y, 'ep', 1, 0, tiled=True)
        out_first = jnp.einsum('gsec,egch->gsh', disp_first, back_y, preferred_element_type=jnp.float32).astype(jnp.bfloat16)
        out_second = jnp.einsum('gsec,egch->gsh', disp_second, back_y, preferred_element_type=jnp.float32).astype(jnp.bfloat16)
        moe_out = norm_first.astype(jnp.float32)[..., None] * out_first + norm_second.astype(jnp.float32)[..., None] * out_second
        dot_sum = jnp.einsum('gsh,gsh->', x_loc, r_loc, preferred_element_type=jnp.float32) + jnp.sum(moe_out * r_loc)
        local_stats = jnp.concatenate([jnp.sum(first_count, axis=0), jnp.sum(router_prob, axis=(0, 1)), dot_sum[None]])
        global_stats = lax.psum(local_stats, 'ep')
        frac_first = global_stats[:experts] / tokens_all
        mean_prob = global_stats[experts:2 * experts] / tokens_all
        loss_value = global_stats[2 * experts] / numel + ALPHA * experts * jnp.sum(frac_first * mean_prob)

        grad_send = jnp.einsum('gsec,gsh->egch', combine, r_loc, preferred_element_type=jnp.float32).astype(jnp.bfloat16)
        grad_y = lax.all_to_all(grad_send, 'ep', 0, 1, tiled=True)
        grad_w_out = jnp.einsum('egcf,egch->efh', act_bf, grad_y, preferred_element_type=jnp.float32).astype(jnp.bfloat16)
        grad_act = jnp.einsum('egch,efh->egcf', grad_y, w_out_loc, preferred_element_type=jnp.float32).astype(jnp.bfloat16)
        grad_pre = act_pull(grad_act)[0].astype(jnp.bfloat16)
        grad_w_in = jnp.einsum('egch,egcf->ehf', expert_x, grad_pre, preferred_element_type=jnp.float32).astype(jnp.bfloat16)
        grad_slots = jnp.einsum('egcf,ehf->egch', grad_pre, w_in_loc, preferred_element_type=jnp.float32).astype(jnp.bfloat16)
        grad_back = lax.all_to_all(grad_slots, 'ep', 1, 0, tiled=True)
        grad_x_moe = jnp.einsum('gsec,egch->gsh', dispatch, grad_back, preferred_element_type=jnp.float32)
        grad_norm_first = jnp.einsum('gsh,gsh->gs', r_loc, out_first, preferred_element_type=jnp.float32).astype(jnp.bfloat16).astype(jnp.float32)
        grad_norm_second = jnp.einsum('gsh,gsh->gs', r_loc, out_second, preferred_element_type=jnp.float32).astype(jnp.bfloat16).astype(jnp.float32)
        gate_sq = gate_sum * gate_sum
        grad_gate_first = (grad_norm_first - grad_norm_second) * gate_second / gate_sq
        grad_gate_second = (grad_norm_second - grad_norm_first) * gate_first / gate_sq
        grad_prob = grad_gate_first[..., None] * first_hot + grad_gate_second[..., None] * second_hot + (ALPHA * hidden * experts) * frac_first
        grad_logits = router_prob * (grad_prob - jnp.sum(router_prob * grad_prob, axis=-1, keepdims=True))
        grad_logits_bf = grad_logits.astype(jnp.bfloat16)
        grad_x_router = jnp.einsum('gse,he->gsh', grad_logits_bf, w_gate, preferred_element_type=jnp.float32)
        grad_x = (r_loc.astype(jnp.float32) + grad_x_moe + grad_x_router).astype(jnp.bfloat16)
        grad_gate_w = lax.psum(jnp.einsum('gsh,gse->he', x_loc, grad_logits_bf, preferred_element_type=jnp.float32), 'ep')
        return loss_value, grad_x, grad_w_in, grad_w_out, grad_gate_w

    row_spec = P('ep', None, None)
    id_spec = P('ep', None)
    return jax.shard_map(layer_body, mesh=mesh, in_specs=(row_spec, row_spec, P(None, None), row_spec, row_spec, id_spec, id_spec, id_spec), out_specs=(P(), row_spec, row_spec, row_spec, P(None, None)), check_vma=False)
```

profile of v0, /device:TPU:0, one launch (start us, length us, event | category | flops | bytes accessed | tf_op | source)
XLA Modules:
  0.0 284.6 jit_solution(17235781442873698965)
XLA Ops:
  7.2 0.0 copy-start
  7.2 0.0 copy-start.2
  7.2 0.9 fusion.51
  8.1 0.7 fusion.92
  8.8 0.7 convert_element_type.170
  9.5 1.3 fusion.95
  10.8 0.2 fusion.112
  11.0 0.7 fusion.90
  11.7 0.9 fusion.109
  12.6 0.9 fusion.52
  13.5 1.3 fusion.39
  14.9 1.5 copy.37
  16.3 7.4 %all-to-all-start = ((bf16[32,4,4,768]{3,2,1,0:T(4,128)(2,1)}), bf16[32,4,4,768]{3,2,1,0:T(4,128)(2,1)S(1)}, u32[]{:S(2)}, u32[]{:S(2)}) async-start(bf16[32,4,4,768]{3,2,1,0:T(4,128)(2,1)} %copy.37), calls=%async_computation | async-start | bytes 1572864 | tf_op jit(solution)/shard_map/all_to_all | solution.py:52
  23.7 1.3 fusion.40
  25.1 1.5 copy.42
  26.6 0.8 fusion.56
  27.4 17.3 %all-to-all-done = bf16[32,4,4,768]{3,2,1,0:T(4,128)(2,1)S(1)} async-done(((bf16[32,4,4,768]{3,2,1,0:T(4,128)(2,1)}), bf16[32,4,4,768]{3,2,1,0:T(4,128)(2,1)S(1)}, u32[]{:S(2)}, u32[]{:S(2)}) %all-to-all-start) | async-done | bytes 786464 | tf_op jit(solution)/shard_map/all_to_all | solution.py:52
  44.7 3.4 %all-to-all-start.2 = ((bf16[32,4,4,768]{3,2,1,0:T(4,128)(2,1)}), bf16[32,4,4,768]{3,2,1,0:T(4,128)(2,1)}, u32[]{:S(2)}, u32[]{:S(2)}) async-start(bf16[32,4,4,768]{3,2,1,0:T(4,128)(2,1)} %copy.42), calls=%async_computation.2 | async-start | bytes 1572864 | tf_op jit(solution)/shard_map/all_to_all | solution.py:68
  48.1 0.0 slice-start.4
  48.1 0.7 copy.46
  48.8 0.0 slice-start.5
  48.8 4.8 %fusion.17 = f32[128,4,3072]{2,0,1:T(8,128)S(1)} fusion(bf16[128,4,768]{0,2,1:T(8,128)(2,1)S(1)} %copy.46, bf16[1,768,3072]{2,1,0:T(8,128)(2,1)} %param.11), kind=kOutput, calls=%fused_computation.24 | convolution fusion | flops 2415919104 | bytes 11796480 | tf_op jit(solution)/shard_map/egch,ehf->egcf/dot_general | solution.py:53
  53.6 3.7 %fusion.32 = bf16[1,128,4,768]{3,1,2,0:T(8,128)(2,1)S(1)} fusion(bf16[1,3072,768]{2,1,0:T(8,128)(2,1)S(1)} %bitcast.130, f32[128,4,3072]{2,0,1:T(8,128)S(1)} %fusion.17), kind=kOutput, calls=%fused_computation.37 | convolution fusion | flops 2430468096 | bytes 11796480 | tf_op jit(solution)/shard_map/egcf,efh->egch/dot_general | solution.py:55
  57.3 1.5 copy.39
  58.9 10.0 %all-to-all-done.2 = bf16[32,4,4,768]{3,2,1,0:T(4,128)(2,1)} async-done(((bf16[32,4,4,768]{3,2,1,0:T(4,128)(2,1)}), bf16[32,4,4,768]{3,2,1,0:T(4,128)(2,1)}, u32[]{:S(2)}, u32[]{:S(2)}) %all-to-all-start.2) | async-done | bytes 786464 | tf_op jit(solution)/shard_map/all_to_all | solution.py:68
  68.9 3.5 %all-to-all-start.1 = ((bf16[1,128,4,768]{3,2,0,1:T(4,128)(2,1)}), bf16[1,128,4,768]{3,2,0,1:T(4,128)(2,1)S(1)}, u32[]{:S(2)}, u32[]{:S(2)}) async-start(bf16[1,128,4,768]{3,2,0,1:T(4,128)(2,1)} %copy.39), calls=%async_computation.1 | async-start | bytes 1572864 | tf_op jit(solution)/shard_map/all_to_all | solution.py:56
  72.4 0.0 slice-start.3
  72.4 8.8 %fusion.3 = bf16[128,4,3072]{2,0,1:T(8,128)(2,1)S(1)} fusion(f32[128,4,3072]{2,0,1:T(8,128)} %copy-done.1, bf16[1,3072,768]{2,1,0:T(8,128)(2,1)} %param.12, bf16[128,4,768]{2,1,0:T(4,128)(2,1)} %bitcast.25), kind=kOutput, calls=%fused_computation.9 | convolution fusion | flops 2450522112 | bytes 14942208 | tf_op jit(solution)/shard_map/egch,efh->egcf/dot_general | solution.py:70
  81.2 2.7 fusion.35
  83.9 1.5 copy.44
  85.4 4.2 %fusion.19 = bf16[1,768,3072]{2,1,0:T(8,128)(2,1)} fusion(bf16[128,4,768]{0,2,1:T(8,128)(2,1)S(1)} %copy.46, bf16[128,4,3072]{2,0,1:T(8,128)(2,1)S(1)} %fusion.3), kind=kOutput, calls=%fused_computation.26 | convolution fusion | flops 2418278400 | bytes 8650752 | tf_op jit(solution)/shard_map/egch,egcf->ehf/dot_general | solution.py:72
  89.6 0.0 copy-start.5
  89.7 6.3 %fusion.20 = bf16[1,3072,768]{2,1,0:T(8,128)(2,1)} fusion(bf16[128,4,768]{2,1,0:T(4,128)(2,1)} %bitcast.25, f32[128,4,3072]{2,0,1:T(8,128)S(1)} %bitcast.122), kind=kOutput, calls=%fused_computation.27 | convolution fusion | flops 2432434176 | bytes 11796480 | tf_op jit(solution)/shard_map/egcf,egch->efh/dot_general | solution.py:69
  96.0 5.7 %all-to-all-start.3 = ((bf16[1,128,4,768]{3,2,0,1:T(4,128)(2,1)}), bf16[1,128,4,768]{3,2,0,1:T(4,128)(2,1)S(1)}, u32[]{:S(2)}, u32[]{:S(2)}) async-start(bf16[1,128,4,768]{3,2,0,1:T(4,128)(2,1)} %copy.44), calls=%async_computation.3 | async-start | bytes 1572864 | tf_op jit(solution)/shard_map/all_to_all | solution.py:74
  101.7 0.0 all-reduce.2.cloned.1.call-start
  101.7 0.4 fusion.44
  102.1 1.2 fusion.54
  104.7 0.1 pad_maximum_fusion
  104.7 40.7 %psum.14 = f32[65]{0:T(128)S(1)} all-reduce(f32[65]{0:T(128)S(1)} %pad_maximum_fusion), channel_id=1, replica_groups=mesh['ep'=32] {'ep'}, use_global_device_ids=true, to_apply=%region_10.0 | all-reduce | flops 65 | bytes 520 | tf_op jit(solution)/shard_map/psum | solution.py:62
  145.5 0.7 slice_multiply_fusion
  146.2 0.1 multiply_reduce_fusion
  146.2 0.9 convolution_bitcast_fusion.3
  147.2 0.0 all-reduce.2.cloned.1.call-update
  147.2 0.3 fusion.93
  147.6 1.2 fusion.41
  148.8 0.6 slice.9
  150.6 124.6 %all-reduce.2.cloned.1.call-done = f32[768,32]{0,1:T(8,128)} async-done(((f32[768,32]{0,1:T(8,128)}), f32[768,32]{0,1:T(8,128)}) %all-reduce.2.cloned.1.call-update) | async-done | bytes 98320 | tf_op jit(solution)/shard_map/psum | solution.py:86
  275.1 1.5 copy.85
  (26 shorter events, 0.1 us)
Async XLA Ops:
  7.2 2.4 copy-start
  7.2 19.4 %copy-start.3 = (bf16[4,64,768]{2,1,0:T(8,128)(2,1)S(1)}, bf16[4,64,768]{2,1,0:T(8,128)(2,1)}, u32[]{:S(2)}) copy-start(bf16[4,64,768]{2,1,0:T(8,128)(2,1)} %param.8) | copy-start | bytes 1179652
  7.2 19.4 %copy-start.2 = (bf16[4,64,768]{2,1,0:T(8,128)(2,1)S(1)}, bf16[4,64,768]{2,1,0:T(8,128)(2,1)}, u32[]{:S(2)}) copy-start(bf16[4,64,768]{2,1,0:T(8,128)(2,1)} %param.9) | copy-start | bytes 1179652
  16.3 28.3 %all-to-all-start = ((bf16[32,4,4,768]{3,2,1,0:T(4,128)(2,1)}), bf16[32,4,4,768]{3,2,1,0:T(4,128)(2,1)S(1)}, u32[]{:S(2)}, u32[]{:S(2)}) async-start(bf16[32,4,4,768]{3,2,1,0:T(4,128)(2,1)} %copy.37), calls=%async_computation | async-start | bytes 1572864 | tf_op jit(solution)/shard_map/all_to_all | solution.py:52
  44.7 24.2 %all-to-all-start.2 = ((bf16[32,4,4,768]{3,2,1,0:T(4,128)(2,1)}), bf16[32,4,4,768]{3,2,1,0:T(4,128)(2,1)}, u32[]{:S(2)}, u32[]{:S(2)}) async-start(bf16[32,4,4,768]{3,2,1,0:T(4,128)(2,1)} %copy.42), calls=%async_computation.2 | async-start | bytes 1572864 | tf_op jit(solution)/shard_map/all_to_all | solution.py:68
  48.1 5.5 %slice-start.4 = ((s8[4718592]{0:T(1024)(128)(4,1)}), s8[524288]{0:T(1024)(128)(4,1)S(1)}, s32[]{:S(2)}) async-start(s8[4718592]{0:T(1024)(128)(4,1)} %bitcast.129), calls=%async_computation.9 | async-start | bytes 1048576
  48.8 4.8 %slice-start.5 = ((s8[4718592]{0:T(1024)(128)(4,1)}), s8[4194304]{0:T(1024)(128)(4,1)S(1)}, s32[]{:S(2)}) async-start(s8[4718592]{0:T(1024)(128)(4,1)} %bitcast.129), calls=%async_computation.10 | async-start | bytes 8388608
  53.6 3.8 %copy-start.1 = (f32[128,4,3072]{2,0,1:T(8,128)}, f32[128,4,3072]{2,0,1:T(8,128)S(1)}, u32[]{:S(2)}) copy-start(f32[128,4,3072]{2,0,1:T(8,128)S(1)} %fusion.17) | copy-start | bytes 18874372
  68.9 12.3 %slice-start.2 = ((s8[4718592]{0:T(1024)(128)(4,1)}), s8[524288]{0:T(1024)(128)(4,1)S(1)}, s32[]{:S(2)}) async-start(s8[4718592]{0:T(1024)(128)(4,1)} %bitcast.123), calls=%async_computation.7 | async-start | bytes 1048576
  68.9 27.1 %all-to-all-start.1 = ((bf16[1,128,4,768]{3,2,0,1:T(4,128)(2,1)}), bf16[1,128,4,768]{3,2,0,1:T(4,128)(2,1)S(1)}, u32[]{:S(2)}, u32[]{:S(2)}) async-start(bf16[1,128,4,768]{3,2,0,1:T(4,128)(2,1)} %copy.39), calls=%async_computation.1 | async-start | bytes 1572864 | tf_op jit(solution)/shard_map/all_to_all | solution.py:56
  72.4 8.8 %slice-start.3 = ((s8[4718592]{0:T(1024)(128)(4,1)}), s8[4194304]{0:T(1024)(128)(4,1)S(1)}, s32[]{:S(2)}) async-start(s8[4718592]{0:T(1024)(128)(4,1)} %bitcast.123), calls=%async_computation.8 | async-start | bytes 8388608
  83.9 5.7 %slice-start = ((s8[6291456]{0:T(1024)(128)(4,1)}), s8[4194304]{0:T(1024)(128)(4,1)S(1)}, s32[]{:S(2)}) async-start(s8[6291456]{0:T(1024)(128)(4,1)} %bitcast.121), calls=%async_computation.5 | async-start | bytes 8388608
  85.4 4.2 %slice-start.1 = ((s8[6291456]{0:T(1024)(128)(4,1)}), s8[2097152]{0:T(1024)(128)(4,1)S(1)}, s32[]{:S(2)}) async-start(s8[6291456]{0:T(1024)(128)(4,1)} %bitcast.121), calls=%async_computation.6 | async-start | bytes 4194304
  89.6 56.5 %copy-start.4 = (s32[4,64]{1,0:T(4,128)S(1)}, s32[4,64]{1,0:T(4,128)}, u32[]{:S(2)}) copy-start(s32[4,64]{1,0:T(4,128)} %param.13) | copy-start | bytes 3076
  89.6 56.5 %copy-start.5 = (s32[4,64]{1,0:T(4,128)S(1)}, s32[4,64]{1,0:T(4,128)}, u32[]{:S(2)}) copy-start(s32[4,64]{1,0:T(4,128)} %param.14) | copy-start | bytes 3076
  96.0 51.6 %all-to-all-start.3 = ((bf16[1,128,4,768]{3,2,0,1:T(4,128)(2,1)}), bf16[1,128,4,768]{3,2,0,1:T(4,128)(2,1)S(1)}, u32[]{:S(2)}, u32[]{:S(2)}) async-start(bf16[1,128,4,768]{3,2,0,1:T(4,128)(2,1)} %copy.44), calls=%async_computation.3 | async-start | bytes 1572864 | tf_op jit(solution)/shard_map/all_to_all | solution.py:74
  101.7 173.5 %all-reduce.2.cloned.1.call-start = ((), (), s32[]{:S(2)}) async-start(), calls=%async_computation.4 | async-start | bytes 196608 | tf_op jit(solution)/shard_map/psum | solution.py:86
Sparse Core Ops, SparseCore 0:
  147.3 127.7 all-reduce.1
where the time goes:
time: 285 us
  waiting for transfers between devices  152 us (53%)
  blocking collectives  40.7 us (14%)
  matrix products  40.4 us (14%)
  starting transfers between devices  19.9 us (7%)
  between operations  18 us (6%)
  local copies, waits for them, and re-layouts  8.88 us (3%)
  other arithmetic  4.84 us (2%)
    psum x1, waiting for transfers between devices, layer_body(): lax.psum(jnp.einsum('gsh,gse->he', x_loc, grad_logits_bf, preferred_eleme...  125 us
    psum x1, blocking collectives, layer_body(): global_stats = lax.psum(local_stats, 'ep')  40.7 us
    all_to_all x1, waiting for transfers between devices, layer_body(): expert_x = lax.all_to_all(send_x, 'ep', 0, 1, tiled=True)  17.3 us
    all_to_all x1, waiting for transfers between devices, layer_body(): grad_y = lax.all_to_all(grad_send, 'ep', 0, 1, tiled=True)  10 us
    dot_general x1, matrix products, layer_body(): jnp.einsum('egch,efh->egcf', grad_y, w_out_loc, preferred_element_type=jn...  8.79 us
    all_to_all x1, starting transfers between devices, layer_body(): expert_x = lax.all_to_all(send_x, 'ep', 0, 1, tiled=True)  7.36 us
    dot_general x1, matrix products, layer_body(): jnp.einsum('egcf,egch->efh', act_bf, grad_y, preferred_element_type=jnp.f...  6.33 us
  transfers between devices with their start and end apart: 5, of which 3 were waited for; matrix products, arithmetic and copies ran while one was open for 15% of the time, Pallas kernels for 0%

commit v1 on v0

--- a/solution.py
+++ b/solution.py
@@ -49,32 +49,34 @@
         dispatch = disp_first + disp_second
         combine = disp_first * norm_first[..., None, None] + disp_second * norm_second[..., None, None]
         send_x = jnp.einsum('gsec,gsh->egch', dispatch, x_loc, preferred_element_type=jnp.float32).astype(jnp.bfloat16)
-        expert_x = lax.all_to_all(send_x, 'ep', 0, 1, tiled=True)
+        send_r = jnp.einsum('gsec,gsh->egch', dispatch, r_loc, preferred_element_type=jnp.float32).astype(jnp.bfloat16)
+        send_n = jnp.einsum('gsec->egc', combine).astype(jnp.bfloat16)
+        send_n = jnp.broadcast_to(send_n[..., None], send_n.shape + (128,))
+        recv = lax.all_to_all(jnp.concatenate([send_x, send_r, send_n], axis=-1), 'ep', 0, 1, tiled=True)
+        expert_x, expert_r, expert_n = recv[..., :hidden], recv[..., hidden:2 * hidden], recv[..., 2 * hidden:2 * hidden + 1]
         pre_act = jnp.einsum('egch,ehf->egcf', expert_x, w_in_loc, preferred_element_type=jnp.float32)
         act_bf, act_pull = jax.vjp(gelu_bf16, pre_act)
         expert_y = jnp.einsum('egcf,efh->egch', act_bf, w_out_loc, preferred_element_type=jnp.float32).astype(jnp.bfloat16)
-        back_y = lax.all_to_all(expert_y, 'ep', 1, 0, tiled=True)
-        out_first = jnp.einsum('gsec,egch->gsh', disp_first, back_y, preferred_element_type=jnp.float32).astype(jnp.bfloat16)
-        out_second = jnp.einsum('gsec,egch->gsh', disp_second, back_y, preferred_element_type=jnp.float32).astype(jnp.bfloat16)
-        moe_out = norm_first.astype(jnp.float32)[..., None] * out_first + norm_second.astype(jnp.float32)[..., None] * out_second
-        dot_sum = jnp.einsum('gsh,gsh->', x_loc, r_loc, preferred_element_type=jnp.float32) + jnp.sum(moe_out * r_loc)
+        dots = jnp.sum(expert_y.astype(jnp.float32) * expert_r.astype(jnp.float32), axis=-1)
+        dot_sum = jnp.einsum('gsh,gsh->', x_loc, r_loc, preferred_element_type=jnp.float32) + jnp.sum(dots * expert_n[..., 0].astype(jnp.float32))
         local_stats = jnp.concatenate([jnp.sum(first_count, axis=0), jnp.sum(router_prob, axis=(0, 1)), dot_sum[None]])
-        global_stats = lax.psum(local_stats, 'ep')
+        global_stats = jnp.sum(lax.optimization_barrier(lax.all_gather(local_stats, 'ep')), axis=0)
         frac_first = global_stats[:experts] / tokens_all
         mean_prob = global_stats[experts:2 * experts] / tokens_all
         loss_value = global_stats[2 * experts] / numel + ALPHA * experts * jnp.sum(frac_first * mean_prob)
 
-        grad_send = jnp.einsum('gsec,gsh->egch', combine, r_loc, preferred_element_type=jnp.float32).astype(jnp.bfloat16)
-        grad_y = lax.all_to_all(grad_send, 'ep', 0, 1, tiled=True)
-        grad_w_out = jnp.einsum('egcf,egch->efh', act_bf, grad_y, preferred_element_type=jnp.float32).astype(jnp.bfloat16)
+        grad_y = (expert_n.astype(jnp.float32) * expert_r.astype(jnp.float32)).astype(jnp.bfloat16)
         grad_act = jnp.einsum('egch,efh->egcf', grad_y, w_out_loc, preferred_element_type=jnp.float32).astype(jnp.bfloat16)
         grad_pre = act_pull(grad_act)[0].astype(jnp.bfloat16)
-        grad_w_in = jnp.einsum('egch,egcf->ehf', expert_x, grad_pre, preferred_element_type=jnp.float32).astype(jnp.bfloat16)
         grad_slots = jnp.einsum('egcf,ehf->egch', grad_pre, w_in_loc, preferred_element_type=jnp.float32).astype(jnp.bfloat16)
         grad_back = lax.all_to_all(grad_slots, 'ep', 1, 0, tiled=True)
+        dots_back = lax.all_to_all(dots, 'ep', 1, 0, tiled=True)
+        grad_w_out = jnp.einsum('egcf,egch->efh', act_bf, grad_y, preferred_element_type=jnp.float32).astype(jnp.bfloat16)
+        grad_w_in = jnp.einsum('egch,egcf->ehf', expert_x, grad_pre, preferred_element_type=jnp.float32).astype(jnp.bfloat16)
         grad_x_moe = jnp.einsum('gsec,egch->gsh', dispatch, grad_back, preferred_element_type=jnp.float32)
-        grad_norm_first = jnp.einsum('gsh,gsh->gs', r_loc, out_first, preferred_element_type=jnp.float32).astype(jnp.bfloat16).astype(jnp.float32)
-        grad_norm_second = jnp.einsum('gsh,gsh->gs', r_loc, out_second, preferred_element_type=jnp.float32).astype(jnp.bfloat16).astype(jnp.float32)
+        dots_slot = jnp.moveaxis(dots_back, 0, 1)[:, None]
+        grad_norm_first = jnp.sum(disp_first * dots_slot, axis=(2, 3)).astype(jnp.bfloat16).astype(jnp.float32)
+        grad_norm_second = jnp.sum(disp_second * dots_slot, axis=(2, 3)).astype(jnp.bfloat16).astype(jnp.float32)
         gate_sq = gate_sum * gate_sum
         grad_gate_first = (grad_norm_first - grad_norm_second) * gate_second / gate_sq
         grad_gate_second = (grad_norm_second - grad_norm_first) * gate_first / gate_sq
@@ -83,7 +85,9 @@
         grad_logits_bf = grad_logits.astype(jnp.bfloat16)
         grad_x_router = jnp.einsum('gse,he->gsh', grad_logits_bf, w_gate, preferred_element_type=jnp.float32)
         grad_x = (r_loc.astype(jnp.float32) + grad_x_moe + grad_x_router).astype(jnp.bfloat16)
-        grad_gate_w = lax.psum(jnp.einsum('gsh,gse->he', x_loc, grad_logits_bf, preferred_element_type=jnp.float32), 'ep')
+        gate_part = jnp.einsum('gsh,gse->he', x_loc, grad_logits_bf, preferred_element_type=jnp.float32)
+        gate_rows = jnp.sum(lax.all_to_all(gate_part.reshape(ep_size, -1, 128), 'ep', 0, 0), axis=0)
+        grad_gate_w = lax.all_gather(gate_rows, 'ep').reshape(hidden, experts)
         return loss_value, grad_x, grad_w_in, grad_w_out, grad_gate_w
 
     row_spec = P('ep', None, None)

time: 285 us -> 217 us (0.76)
  waiting for transfers between devices: 152 us -> 39.8 us
  blocking collectives: 40.7 us -> 82.6 us
  between operations: 18 us -> 4.62 us
  matrix products: 40.4 us -> 51.2 us
    psum x1 -> x0, waiting for transfers between devices: 125 us -> none  [layer_body(): lax.psum(jnp.einsum('gsh,gse->he', x_loc, grad_logits_bf, preferred_eleme...]
    all_gather x0 -> x1, blocking collectives: none -> 41.9 us  [layer_body(): grad_gate_w = lax.all_gather(gate_rows, 'ep').reshape(hidden, experts)]
    unnamed x0 -> x1, blocking collectives: none -> 40.7 us
    psum x1 -> x0, blocking collectives: 40.7 us -> none  [layer_body(): global_stats = lax.psum(local_stats, 'ep')]
    all_to_all x3, waiting for transfers between devices: 27.3 us -> 39.8 us  [the longest x1 39.8 us: layer_body(): lax.all_to_all(jnp.concatenate([send_x, send_r, send_n], axis=-1), 'ep',...]
    dot_general x1, matrix products: 3.74 us -> 8.44 us  [layer_body(): jnp.einsum('egcf,efh->egch', act_bf, w_out_loc, preferred_element_type=jn...]
    convert_element_type x3 -> x0, local copies, waits for them, and re-layouts: 4.53 us -> none  [the longest x1 1.55 us: layer_body(): jnp.einsum('egcf,efh->egch', act_bf, w_out_loc, preferred_element_type=jn...]
    dot_general x1, matrix products: 2.66 us -> 5.99 us  [layer_body(): jnp.einsum('egcf,ehf->egch', grad_pre, w_in_loc, preferred_element_type=j...]
  transfers between devices with their start and end apart: 5 -> 4, of which waited for: 3 -> 1; matrix products, arithmetic and copies ran while one was open for 15% -> 16% of each run, Pallas kernels for 0% -> 0%
where the time goes in v1:
time: 217 us; the launch traced here: 216 us
  blocking collectives  82.6 us (38%)
  matrix products  51.2 us (24%)
  waiting for transfers between devices  39.8 us (18%)
  starting transfers between devices  21.1 us (10%)
  local copies, waits for them, and re-layouts  10.6 us (5%)
  other arithmetic  6.13 us (3%)
  between operations  4.62 us (2%)
    all_gather x1, blocking collectives, layer_body(): grad_gate_w = lax.all_gather(gate_rows, 'ep').reshape(hidden, experts)  41.9 us
    unnamed x1, blocking collectives  40.7 us
    all_to_all x1, waiting for transfers between devices, layer_body(): lax.all_to_all(jnp.concatenate([send_x, send_r, send_n], axis=-1), 'ep',...  39.8 us
    dot_general x1, matrix products, layer_body(): jnp.einsum('egch,efh->egcf', grad_y, w_out_loc, preferred_element_type=jn...  9.88 us
    dot_general x1, matrix products, layer_body(): jnp.einsum('egcf,efh->egch', act_bf, w_out_loc, preferred_element_type=jn...  8.44 us
    dot_general x1, matrix products, layer_body(): jnp.einsum('egcf,egch->efh', act_bf, grad_y, preferred_element_type=jnp.f...  8.36 us
    all_to_all x1, starting transfers between devices, layer_body(): lax.all_to_all(jnp.concatenate([send_x, send_r, send_n], axis=-1), 'ep',...  7.37 us
    dot_general x1, matrix products, layer_body(): jnp.einsum('egch,egcf->ehf', expert_x, grad_pre, preferred_element_type=j...  6.18 us
  transfers between devices with their start and end apart: 4, of which 1 were waited for; matrix products, arithmetic and copies ran while one was open for 16% of the time, Pallas kernels for 0%

profile of v1, /device:TPU:0, one launch (start us, length us, event | category | flops | bytes accessed | tf_op | source)
XLA Modules:
  0.0 216.1 jit_solution(5599936543001441047)
XLA Ops:
  0.6 0.9 fusion.50
  1.6 0.7 fusion.81
  2.3 1.3 fusion.84
  3.5 0.2 fusion.100
  3.7 0.7 convert_element_type.188
  4.4 0.7 fusion.74
  5.1 0.9 fusion.98
  6.0 0.9 fusion.51
  7.0 1.4 fusion.42
  8.4 1.3 fusion.43
  9.7 0.2 fusion.62
  9.9 0.1 broadcast_in_dim.4
  10.0 0.2 pad_maximum_fusion
  10.2 2.1 copy.52
  12.3 7.4 %all-to-all-start = ((bf16[32,4,4,1664]{3,2,1,0:T(4,128)(2,1)}), bf16[32,4,4,1664]{3,2,1,0:T(4,128)(2,1)S(1)}, u32[]{:S(2)}, u32[]{:S(2)}) async-start(bf16[32,4,4,1664]{3,2,1,0:T(4,128)(2,1)} %copy.52), calls=%async_computation | async-start | bytes 3407872 | tf_op jit(solution)/shard_map/all_to_all | solution.py:55
  19.7 0.8 fusion.55
  20.5 39.8 %all-to-all-done = bf16[32,4,4,1664]{3,2,1,0:T(4,128)(2,1)S(1)} async-done(((bf16[32,4,4,1664]{3,2,1,0:T(4,128)(2,1)}), bf16[32,4,4,1664]{3,2,1,0:T(4,128)(2,1)S(1)}, u32[]{:S(2)}, u32[]{:S(2)}) %all-to-all-start) | async-done | bytes 1703968 | tf_op jit(solution)/shard_map/all_to_all | solution.py:55
  60.3 1.4 fusion.99
  61.7 0.7 slice.26
  62.4 1.0 copy.80
  63.5 4.7 %fusion.17 = f32[128,4,3072]{2,0,1:T(8,128)S(1)} fusion(bf16[1,768,3072]{2,1,0:T(8,128)(2,1)} %param.11, bf16[1,128,4,768]{3,2,1,0:T(4,128)(2,1)} %get-tuple-element.32), kind=kOutput, calls=%fused_computation.24 | convolution fusion | flops 2415919104 | bytes 11796480 | tf_op jit(solution)/shard_map/egch,ehf->egcf/dot_general | solution.py:57
  68.2 8.4 %fusion.26 = f32[128,4]{0,1:T(4,128)S(1)} fusion(bf16[1,3072,768]{2,1,0:T(8,128)(2,1)} %param.12, bf16[1,128,4,768]{3,2,1,0:T(4,128)(2,1)S(1)} %get-tuple-element.33, f32[128,4,3072]{2,0,1:T(8,128)S(1)} %fusion.17), kind=kOutput, calls=%fused_computation.32 | convolution fusion | flops 2432040448 | bytes 11798528 | tf_op jit(solution)/shard_map/egcf,efh->egch/dot_general | solution.py:59
  76.6 0.6 multiply_reduce_fusion.3
  77.2 0.7 copy.58
  77.9 3.1 %all-to-all-start.2 = ((f32[1,128,4]{2,0,1:T(1,128)}), f32[1,128,4]{2,0,1:T(1,128)S(1)}, u32[]{:S(2)}, u32[]{:S(2)}) async-start(f32[1,128,4]{2,0,1:T(1,128)} %copy.58), calls=%async_computation.2 | async-start | bytes 131072 | tf_op jit(solution)/shard_map/all_to_all | solution.py:73
  82.4 0.2 maximum_dynamic-update-slice_fusion
  82.6 40.7 %all-reduce = f32[2080]{0:T(1024)S(1)} all-reduce(f32[2080]{0:T(1024)S(1)} %maximum_dynamic-update-slice_fusion), channel_id=2, replica_groups=mesh['ep'=32] {'ep'}, use_global_device_ids=true, to_apply=%add | all-reduce | flops 2080 | bytes 16640
  123.3 0.1 reshape.192
  123.5 9.9 %fusion.3 = bf16[128,4,3072]{2,0,1:T(8,128)(2,1)} fusion(f32[128,4,3072]{2,0,1:T(8,128)} %copy-done.6, bf16[1,3072,768]{2,1,0:T(8,128)(2,1)} %param.12, f32[128,4]{0,1:T(4,128)S(1)} %bitcast_convert_fusion.2, bf16[1,128,4,768]{3,2,1,0:T(4,128)(2,1)S(1)} %get-tuple-element.33), kind=kOutput, calls=%fused_computation.9 | convolution fusion | flops 2451701760 | bytes 14944256 | tf_op jit(solution)/shard_map/egch,efh->egcf/dot_general | solution.py:69
  133.3 0.7 slice_multiply_fusion
  134.0 0.3 copy.77
  134.5 0.2 multiply_reduce_fusion.1
  134.7 0.1 multiply_reduce_fusion.2
  134.8 0.3 convolution_bitcast_fusion.1
  135.1 0.2 copy.63
  135.2 0.8 reshape.188
  136.0 4.5 %all-to-all-start.3 = ((f32[32,6,128]{2,1,0:T(8,128)}), f32[32,6,128]{2,1,0:T(8,128)S(1)}, u32[]{:S(2)}, u32[]{:S(2)}) async-start(f32[32,6,128]{2,1,0:T(8,128)} %reshape.188), calls=%async_computation.3 | async-start | bytes 262144 | tf_op jit(solution)/shard_map/all_to_all | solution.py:89
  140.6 6.0 %fusion.37 = bf16[1,128,4,768]{3,1,2,0:T(8,128)(2,1)S(1)} fusion(bf16[128,4,3072]{2,0,1:T(8,128)(2,1)} %fusion.3, bf16[1,768,3072]{2,1,0:T(8,128)(2,1)} %param.11), kind=kOutput, calls=%fused_computation.39 | convolution fusion | flops 2416312320 | bytes 8650752 | tf_op jit(solution)/shard_map/egcf,ehf->egch/dot_general | solution.py:71
  146.6 0.6 slice.21
  147.2 1.5 copy.56
  150.0 6.1 %all-to-all-start.1 = ((bf16[1,128,4,768]{3,2,0,1:T(4,128)(2,1)}), bf16[1,128,4,768]{3,2,0,1:T(4,128)(2,1)S(1)}, u32[]{:S(2)}, u32[]{:S(2)}) async-start(bf16[1,128,4,768]{3,2,0,1:T(4,128)(2,1)} %copy.56), calls=%async_computation.1 | async-start | bytes 1572864 | tf_op jit(solution)/shard_map/all_to_all | solution.py:72
  156.0 6.2 %fusion.19 = bf16[1,768,3072]{2,1,0:T(8,128)(2,1)} fusion(bf16[128,4,3072]{2,0,1:T(8,128)(2,1)} %fusion.3, bf16[1,128,4,768]{3,2,1,0:T(4,128)(2,1)S(1)} %copy-done.3), kind=kOutput, calls=%fused_computation.26 | convolution fusion | flops 2418278400 | bytes 8650752 | tf_op jit(solution)/shard_map/egch,egcf->ehf/dot_general | solution.py:75
  162.2 8.4 %fusion.20 = bf16[1,3072,768]{2,1,0:T(8,128)(2,1)} fusion(f32[128,4]{0,1:T(4,128)S(1)} %bitcast_convert_fusion.2, bf16[1,128,4,768]{3,2,1,0:T(4,128)(2,1)S(1)} %get-tuple-element.33, f32[128,4,3072]{2,0,1:T(8,128)} %copy-done.6), kind=kOutput, calls=%fused_computation.27 | convolution fusion | flops 2433613824 | bytes 11798528 | tf_op jit(solution)/shard_map/egcf,egch->efh/dot_general | solution.py:74
  170.6 0.3 fusion.82
  171.0 41.9 %all-gather.2 = f32[32,6,128]{2,1,0:T(8,128)S(1)} all-gather(f32[1,6,128]{2,1,0:T(8,128)S(1)} %bitcast.132), channel_id=3, replica_groups=mesh['ep'=32] {'ep'}, dimensions={0}, use_global_device_ids=true | all-gather | bytes 101376 | tf_op jit(solution)/shard_map/all_gather | solution.py:90
  212.9 0.1 reshape.189
  213.0 0.8 copy.64
  213.8 1.2 fusion.44
  (25 shorter events, 0.2 us)
Async XLA Ops:
  0.6 1.6 copy-start
  6.9 12.7 %copy-start.1 = (bf16[4,64,768]{2,1,0:T(8,128)(2,1)S(1)}, bf16[4,64,768]{2,1,0:T(8,128)(2,1)}, u32[]{:S(2)}) copy-start(bf16[4,64,768]{2,1,0:T(8,128)(2,1)} %param.9) | copy-start | bytes 1179652
  7.0 12.7 %copy-start.2 = (bf16[4,64,768]{2,1,0:T(8,128)(2,1)S(1)}, bf16[4,64,768]{2,1,0:T(8,128)(2,1)}, u32[]{:S(2)}) copy-start(bf16[4,64,768]{2,1,0:T(8,128)(2,1)} %param.8) | copy-start | bytes 1179652
  12.3 48.1 %all-to-all-start = ((bf16[32,4,4,1664]{3,2,1,0:T(4,128)(2,1)}), bf16[32,4,4,1664]{3,2,1,0:T(4,128)(2,1)S(1)}, u32[]{:S(2)}, u32[]{:S(2)}) async-start(bf16[32,4,4,1664]{3,2,1,0:T(4,128)(2,1)} %copy.52), calls=%async_computation | async-start | bytes 3407872 | tf_op jit(solution)/shard_map/all_to_all | solution.py:55
  68.1 8.4 %copy-start.6 = (f32[128,4,3072]{2,0,1:T(8,128)}, f32[128,4,3072]{2,0,1:T(8,128)S(1)}, u32[]{:S(2)}) copy-start(f32[128,4,3072]{2,0,1:T(8,128)S(1)} %fusion.17) | copy-start | bytes 18874372
  77.9 56.1 %all-to-all-start.2 = ((f32[1,128,4]{2,0,1:T(1,128)}), f32[1,128,4]{2,0,1:T(1,128)S(1)}, u32[]{:S(2)}, u32[]{:S(2)}) async-start(f32[1,128,4]{2,0,1:T(1,128)} %copy.58), calls=%async_computation.2 | async-start | bytes 131072 | tf_op jit(solution)/shard_map/all_to_all | solution.py:73
  123.4 11.2 %copy-start.4 = (s32[4,64]{1,0:T(4,128)S(1)}, s32[4,64]{1,0:T(4,128)}, u32[]{:S(2)}) copy-start(s32[4,64]{1,0:T(4,128)} %param.13) | copy-start | bytes 3076
  123.5 11.2 %copy-start.5 = (s32[4,64]{1,0:T(4,128)S(1)}, s32[4,64]{1,0:T(4,128)}, u32[]{:S(2)}) copy-start(s32[4,64]{1,0:T(4,128)} %param.14) | copy-start | bytes 3076
  136.0 13.9 %all-to-all-start.3 = ((f32[32,6,128]{2,1,0:T(8,128)}), f32[32,6,128]{2,1,0:T(8,128)S(1)}, u32[]{:S(2)}, u32[]{:S(2)}) async-start(f32[32,6,128]{2,1,0:T(8,128)} %reshape.188), calls=%async_computation.3 | async-start | bytes 262144 | tf_op jit(solution)/shard_map/all_to_all | solution.py:89
  140.6 15.5 %copy-start.3 = (bf16[1,128,4,768]{3,2,1,0:T(4,128)(2,1)S(1)}, bf16[1,128,4,768]{3,2,1,0:T(4,128)(2,1)}, u32[]{:S(2)}) copy-start(bf16[1,128,4,768]{3,2,1,0:T(4,128)(2,1)} %get-tuple-element.32) | copy-start | bytes 2359300
  150.0 63.8 %all-to-all-start.1 = ((bf16[1,128,4,768]{3,2,0,1:T(4,128)(2,1)}), bf16[1,128,4,768]{3,2,0,1:T(4,128)(2,1)S(1)}, u32[]{:S(2)}, u32[]{:S(2)}) async-start(bf16[1,128,4,768]{3,2,0,1:T(4,128)(2,1)} %copy.56), calls=%async_computation.1 | async-start | bytes 1572864 | tf_op jit(solution)/shard_map/all_to_all | solution.py:72

commit v2 on v0

v2 whole, which is shorter than its diff:
```python
import functools

import jax
import jax.numpy as jnp
from jax import lax
from jax.experimental import pallas as pl
from jax.experimental.pallas import tpu as pltpu
from jax.sharding import PartitionSpec as P

ALPHA = 0.01
MESH = pl.DeviceIdType.MESH
F32 = jnp.float32
BF16 = jnp.bfloat16
NN = (((1,), (0,)), ((), ()))
NT = (((1,), (1,)), ((), ()))
TN = (((0,), (0,)), ((), ()))
GELU_C = 0.7978845608028654
GELU_K = 0.044715


def dot(a, b, dims=NN, **kw):
    return lax.dot_general(a, b, dims, preferred_element_type=F32, **kw)


def iota(shape, dim):
    return lax.broadcasted_iota(jnp.int32, shape, dim)


def flip_bits(a, b):
    return a + b - 2 * a * b


def layer_kernel(n, cap, seq, ids_ref, x_ref, r_ref, wg_ref, w1_hbm, w2_hbm,
                 loss_ref, gx_ref, gg_ref, gw1_hbm, gw2_hbm,
                 w1, w2, sx, sr, xe, re, gy, act, gpre, gs, gback, rows_s, rows_r, dots_s, dots_r,
                 part_s, part_r, sum_s, hacc, gacc, xet, stage1, stage2,
                 w_sem, out_sem, s_x, s_r, s_g, s_row, s_dot, s_part, s_sum,
                 v_x, v_r, v_g, v_row, v_dot, v_part, v_sum):
    me = lax.axis_index('ep')
    tokens, hidden = x_ref.shape
    ff = w1.shape[1]
    groups = tokens // seq
    rows = groups * cap
    slots = n * rows
    half = slots // 2
    plane = n // 4
    tokens_all = tokens * n
    numel = tokens_all * hidden
    tile = 512
    tiles = ff // tile

    low, high = lax.rem(me, plane), lax.div(me, plane)
    low_bits = [lax.rem(low, 2), lax.rem(lax.div(low, 2), 2), lax.div(low, 4)]
    high_bits = [lax.rem(high, 2), lax.div(high, 2)]
    order = (0, 2, 1, 3)

    def partner(quarter, step):
        far = order[quarter]
        top = [bit if not (far >> i) & 1 else 1 - bit for i, bit in enumerate(high_bits)]
        step_bits = [lax.rem(step, 2), lax.rem(lax.div(step, 2), 2), lax.div(step, 4)]
        bits = [flip_bits(a, b) for a, b in zip(low_bits, step_bits)]
        return (top[0] + 2 * top[1]) * plane + bits[0] + 2 * bits[1] + 4 * bits[2]

    def each_partner(quarters, body):
        for quarter in quarters:
            first = 1 if quarter == 0 else 0

            @pl.loop(first, plane)
            def _(step):
                body(quarter * plane + step, partner(quarter, step))

    everyone = (0, 1, 2, 3)
    quarters_of = ((0, 1), (2, 3))

    barrier = pltpu.get_barrier_semaphore()
    each_partner(everyone, lambda q, d: pl.semaphore_signal(barrier, inc=1, device_id=(d,), device_id_type=MESH))
    w1_copy = pltpu.make_async_copy(w1_hbm, w1, w_sem.at[0])
    w2_copy = pltpu.make_async_copy(w2_hbm, w2, w_sem.at[1])
    w1_copy.start()
    w2_copy.start()

    e1, e2, k2 = ids_ref[0:1, :], ids_ref[1:2, :], ids_ref[2:3, :]
    row_i, col_i = iota((tokens, tokens), 0), iota((tokens, tokens), 1)
    eye = row_i == col_i

    def column(row):
        return jnp.sum(jnp.where(eye, row, 0), axis=1, keepdims=True)

    e1c, e2c, k2c = column(e1), column(e2), column(k2)
    same_group = (row_i // seq) == (col_i // seq)
    earlier = same_group & (row_i < col_i)
    one = jnp.int32(1)
    pos1 = jnp.sum(jnp.where(earlier & (e1c == e1), one, 0), axis=0, keepdims=True)
    count1 = jnp.sum(jnp.where(same_group & (e1c == e2), one, 0), axis=0, keepdims=True)
    before2 = jnp.sum(jnp.where(earlier & (e2c == e2) & (k2c > 0), one, 0), axis=0, keepdims=True)
    pos2 = count1 + before2
    lane = iota((1, tokens), 1)
    group_base = (lane // seq) * cap
    kept1 = pos1 < cap
    kept2 = (pos2 < cap) & (k2 > 0)
    place1 = jnp.where(kept1, group_base + pos1, -1)
    place2 = jnp.where(kept2, group_base + pos2, -1)

    def slot_of(expert):
        apart = expert ^ me
        top = apart // plane
        swapped = (top // 2) + 2 * (top % 2)
        return swapped * plane + apart % plane

    key1 = jnp.where(kept1, slot_of(e1) * rows + place1, -1)
    key2 = jnp.where(kept2, slot_of(e2) * rows + place2, -1)
    slot_i = iota((slots, tokens), 0)
    disp = ((slot_i == key1) | (slot_i == key2)).astype(F32).astype(BF16)

    expert_i = iota((n, tokens), 0)
    hot1 = (expert_i == e1).astype(F32)
    hot2 = (expert_i == e2).astype(F32)
    place_i = iota((128, tokens), 0)
    at1 = (place_i == place1).astype(F32)
    at2 = (place_i == place2).astype(F32)

    x = x_ref[...]
    r = r_ref[...]
    wgt = wg_ref[...]
    logits = dot(wgt, x, NT)
    top_logit = jnp.max(logits, axis=0, keepdims=True)
    expd = jnp.exp(logits - top_logit)
    prob = expd / jnp.sum(expd, axis=0, keepdims=True)
    g1 = jnp.sum(prob * hot1, axis=0, keepdims=True)
    g2 = jnp.sum(prob * hot2, axis=0, keepdims=True)
    gsum = g1 + g2
    n1 = (g1 / gsum).astype(BF16).astype(F32)
    n2 = (g2 / gsum).astype(BF16).astype(F32)
    norm_rows = dot((hot1 * n1).astype(BF16), at1.astype(BF16), NT) + dot((hot2 * n2).astype(BF16), at2.astype(BF16), NT)
    sub_n, lane_n = iota((n, 128), 0), iota((n, 128), 1)

    def as_lanes(col, base):
        return jnp.sum(jnp.where(lane_n == sub_n + base, col, 0.0), axis=0, keepdims=True)

    def as_column(row, base):
        return jnp.sum(jnp.where(lane_n == sub_n + base, row, 0.0), axis=1, keepdims=True)

    xr = jnp.sum(jnp.sum(x.astype(F32) * r.astype(F32), axis=0, keepdims=True), axis=1, keepdims=True)
    lane_1 = iota((1, 128), 1)
    stats = as_lanes(jnp.sum(hot1, axis=1, keepdims=True), 32) + as_lanes(jnp.sum(prob, axis=1, keepdims=True), 64) + jnp.where(lane_1 == 96, xr, 0.0)
    rows_s[...] = norm_rows + stats

    sx[...] = dot(disp, x).astype(BF16)
    sr[...] = dot(disp, r).astype(BF16)

    pl.semaphore_wait(barrier, n - 1)

    def one_row(src, dst, src_row, send, recv, q, d):
        return pltpu.make_async_remote_copy(src.at[pl.ds(src_row, 1)], dst.at[pl.ds(me, 1)], send.at[q], recv.at[0], device_id=(d,), device_id_type=MESH)

    def block(src, dst, send, recv, half_i, q, d):
        at = pl.ds(q * rows, rows)
        return pltpu.make_async_remote_copy(src.at[at], dst.at[at], send.at[half_i], recv.at[half_i], device_id=(d,), device_id_type=MESH)

    def own_row(src, dst, src_row, recv):
        pltpu.make_async_copy(src.at[pl.ds(src_row, 1)], dst.at[pl.ds(me, 1)], recv.at[0]).start()

    def own_block(src, dst, recv):
        pltpu.make_async_copy(src.at[pl.ds(0, rows)], dst.at[pl.ds(0, rows)], recv.at[0]).start()

    def settle(ref, sem, rows_at):
        pltpu.make_async_copy(ref.at[rows_at], ref.at[rows_at], sem).wait()

    def half_at(c):
        return pl.ds(c * half, half)

    each_partner(everyone, lambda q, d: one_row(rows_s, rows_r, d, s_row, v_row, q, d).start())
    own_row(rows_s, rows_r, me, v_row)
    own_block(sx, xe, v_x)
    own_block(sr, re, v_r)
    for c in range(2):
        each_partner(quarters_of[c], lambda q, d: block(sx, xe, s_x, v_x, c, q, d).start())
        each_partner(quarters_of[c], lambda q, d: block(sr, re, s_r, v_r, c, q, d).start())

    settle(rows_r, v_row.at[0], pl.ds(0, n))
    all_rows = rows_r[...]
    total = jnp.sum(all_rows, axis=0, keepdims=True)
    frac = as_column(total, 32) / tokens_all
    mean_prob = as_column(total, 64) / tokens_all
    w1_copy.wait()
    w2_copy.wait()

    loss_part = jnp.zeros((1, 1), F32)
    for c in range(2):
        at = half_at(c)
        settle(xe, v_x.at[c], at)
        settle(re, v_r.at[c], at)
        slot_row = iota((half, n), 0) + c * half
        apart = slot_row // rows
        top = apart // plane
        source = (((top // 2) + 2 * (top % 2)) * plane + apart % plane) ^ me
        pick = (source == iota((half, n), 1)).astype(F32).astype(BF16)
        wide = dot(pick, all_rows.astype(BF16))
        mine = iota((half, 128), 1) == iota((half, 128), 0) % rows
        norm = jnp.sum(jnp.where(mine, wide, 0.0), axis=1, keepdims=True)
        xc = xe[at, :]
        rc = re[at, :].astype(F32)
        gy[at, :] = (norm * rc).astype(BF16)
        hacc[...] = jnp.zeros_like(hacc)
        gacc[...] = jnp.zeros_like(gacc)

        @pl.loop(0, tiles)
        def _(f):
            cols = pl.ds(pl.multiple_of(f * tile, tile), tile)
            w1t = w1[:, cols]
            w2t = w2[cols, :]
            pre = dot(xe[at, :], w1t)
            sq = pre * pre
            th = jnp.tanh(GELU_C * (pre + GELU_K * (sq * pre)))
            cdf = 0.5 * (1.0 + th)
            a = (pre * cdf).astype(BF16)
            slope = cdf + (0.5 * GELU_C) * pre * (1.0 - th * th) * (1.0 + 3 * GELU_K * sq)
            act[at, cols] = a
            hacc[...] += dot(a, w2t)
            ga = dot(gy[at, :], w2t, NT).astype(BF16)
            gp = (ga.astype(F32) * slope).astype(BF16)
            gpre[at, cols] = gp
            gacc[...] += dot(gp, w1t, NT)

        h = hacc[...].astype(BF16).astype(F32)
        d = jnp.sum(h * rc, axis=1, keepdims=True)
        loss_part = loss_part + jnp.sum(norm * d, axis=0, keepdims=True)
        spread = jnp.where(mine, d, 0.0)
        dots_s[pl.ds(c * (n // 2), n // 2), :] = jnp.sum(spread.reshape(n // 2, rows, 128), axis=1)
        gs[at, :] = gacc[...].astype(BF16)
        if c == 1:
            dots_s[...] = dots_s[...] + jnp.where(lane_1 == 16, loss_part, 0.0)
            each_partner(everyone, lambda q, d: one_row(dots_s, dots_r, q, s_dot, v_dot, q, d).start())
            own_row(dots_s, dots_r, 0, v_dot)
        else:
            own_block(gs, gback, v_g)
        each_partner(quarters_of[c], lambda q, d: block(gs, gback, s_g, v_g, c, q, d).start())

    def put1(f, slot):
        cols = pl.ds(pl.multiple_of(f * tile, tile), tile)
        return pltpu.make_async_copy(stage1.at[slot], gw1_hbm.at[:, cols], out_sem.at[slot])

    def put2(f, slot):
        cols = pl.ds(pl.multiple_of(f * tile, tile), tile)
        return pltpu.make_async_copy(stage2.at[slot], gw2_hbm.at[cols, :], out_sem.at[2 + slot])

    xet[...] = jnp.transpose(xe[...])

    @pl.loop(0, tiles)
    def _(f):
        slot = lax.rem(f, 2)

        @pl.when(f >= 2)
        def _():
            put1(f - 2, slot).wait()

        cols = pl.ds(pl.multiple_of(f * tile, tile), tile)
        stage1[slot] = dot(xet[...], gpre[:, cols]).astype(BF16)
        put1(f, slot).start()

    settle(dots_r, v_dot.at[0], pl.ds(0, n))
    all_dots = dots_r[...]
    exact = lax.Precision.HIGHEST
    d1 = jnp.sum(dot(all_dots, hot1, TN, precision=exact) * at1, axis=0, keepdims=True)
    d2 = jnp.sum(dot(all_dots, hot2, TN, precision=exact) * at2, axis=0, keepdims=True)
    d1 = d1.astype(BF16).astype(F32)
    d2 = d2.astype(BF16).astype(F32)
    gate_sq = gsum * gsum
    up1 = (d1 - d2) * g2 / gate_sq
    up2 = (d2 - d1) * g1 / gate_sq
    gprob = up1 * hot1 + up2 * hot2 + (ALPHA * hidden * n) * frac
    glog = (prob * (gprob - jnp.sum(prob * gprob, axis=0, keepdims=True))).astype(BF16)
    part_s[...] = dot(glog, x)
    each_partner(everyone, lambda q, d: one_row(part_s, part_r, d, s_part, v_part, q, d).start())
    own_row(part_s, part_r, me, v_part)

    both = jnp.sum(jnp.where(lane_1 == 96, total, 0.0), axis=1, keepdims=True)
    both = both + jnp.sum(jnp.where(lane_1 == 16, jnp.sum(all_dots, axis=0, keepdims=True), 0.0), axis=1, keepdims=True)
    aux = jnp.sum(frac * mean_prob, axis=0, keepdims=True) * n
    loss_ref[...] = jnp.broadcast_to(both / numel + ALPHA * aux, loss_ref.shape)

    @pl.loop(0, tiles)
    def _(f):
        slot = lax.rem(f, 2)

        @pl.when(f >= 2)
        def _():
            put2(f - 2, slot).wait()

        cols = pl.ds(pl.multiple_of(f * tile, tile), tile)
        stage2[slot] = dot(act[:, cols], gy[...], TN).astype(BF16)
        put2(f, slot).start()

    settle(part_r, v_part.at[0], pl.ds(0, n))
    sum_s[0:1, :] = jnp.sum(part_r[...], axis=0, keepdims=True)
    each_partner(everyone, lambda q, d: one_row(sum_s, gg_ref, 0, s_sum, v_sum, q, d).start())
    own_row(sum_s, gg_ref, 0, v_sum)

    key1c, key2c = column(key1), column(key2)
    slot_l = iota((tokens, slots), 1)
    comb = ((slot_l == key1c) | (slot_l == key2c)).astype(F32).astype(BF16)
    near = r.astype(F32) + dot(glog, wgt, TN)
    for c in range(2):
        settle(gback, v_g.at[c], half_at(c))
    gx_ref[...] = (near + dot(comb, gback[...])).astype(BF16)

    settle(gg_ref, v_sum.at[0], pl.ds(0, n))
    for f in range(tiles - 2, tiles):
        put1(f, f % 2).wait()
        put2(f, f % 2).wait()
    each_partner(everyone, lambda q, d: one_row(rows_s, rows_r, d, s_row, v_row, q, d).wait_send())
    each_partner(everyone, lambda q, d: one_row(dots_s, dots_r, q, s_dot, v_dot, q, d).wait_send())
    each_partner(everyone, lambda q, d: one_row(part_s, part_r, d, s_part, v_part, q, d).wait_send())
    each_partner(everyone, lambda q, d: one_row(sum_s, gg_ref, 0, s_sum, v_sum, q, d).wait_send())
    for ref, sem in ((sx, s_x), (sr, s_r), (gs, s_g)):
        settle(ref, sem.at[0], pl.ds(rows, half - rows))
        settle(ref, sem.at[1], half_at(1))


def solution(mesh):
    n = mesh.shape['ep']

    def layer_body(x_loc, r_loc, w_gate, w_in_loc, w_out_loc, first_ids, second_ids, keep_ids):
        groups, seq, hidden = x_loc.shape
        cap = 2 * seq // w_gate.shape[1]
        ff = w_in_loc.shape[2]
        tokens = groups * seq
        slots = n * groups * cap
        tile = 512
        ids = jnp.concatenate([first_ids.reshape(1, tokens), second_ids.reshape(1, tokens), keep_ids.reshape(1, tokens), jnp.zeros((5, tokens), jnp.int32)])
        vmem = pl.BlockSpec(memory_space=pltpu.VMEM)
        hbm = pl.BlockSpec(memory_space=pl.ANY)
        dma = pltpu.SemaphoreType.DMA
        out = pl.pallas_call(
            functools.partial(layer_kernel, n, cap, seq),
            name='moe_layer',
            out_shape=(
                jax.ShapeDtypeStruct((8, 128), F32),
                jax.ShapeDtypeStruct((tokens, hidden), BF16),
                jax.ShapeDtypeStruct((n, hidden), F32),
                jax.ShapeDtypeStruct((hidden, ff), BF16),
                jax.ShapeDtypeStruct((ff, hidden), BF16),
            ),
            in_specs=[vmem, vmem, vmem, vmem, hbm, hbm],
            out_specs=(vmem, vmem, vmem, hbm, hbm),
            scratch_shapes=[
                pltpu.VMEM((hidden, ff), BF16),
                pltpu.VMEM((ff, hidden), BF16),
                pltpu.VMEM((slots, hidden), BF16),
                pltpu.VMEM((slots, hidden), BF16),
                pltpu.VMEM((slots, hidden), BF16),
                pltpu.VMEM((slots, hidden), BF16),
                pltpu.VMEM((slots, hidden), BF16),
                pltpu.VMEM((slots, ff), BF16),
                pltpu.VMEM((slots, ff), BF16),
                pltpu.VMEM((slots, hidden), BF16),
                pltpu.VMEM((slots, hidden), BF16),
                pltpu.VMEM((n, 128), F32),
                pltpu.VMEM((n, 128), F32),
                pltpu.VMEM((n, 128), F32),
                pltpu.VMEM((n, 128), F32),
                pltpu.VMEM((n, hidden), F32),
                pltpu.VMEM((n, hidden), F32),
                pltpu.VMEM((8, hidden), F32),
                pltpu.VMEM((slots // 2, hidden), F32),
                pltpu.VMEM((slots // 2, hidden), F32),
                pltpu.VMEM((hidden, slots), BF16),
                pltpu.VMEM((2, hidden, tile), BF16),
                pltpu.VMEM((2, tile, hidden), BF16),
                dma((2,)), dma((4,)),
                dma((2,)), dma((2,)), dma((2,)), dma((n,)), dma((n,)), dma((n,)), dma((n,)),
                dma((2,)), dma((2,)), dma((2,)), dma((1,)), dma((1,)), dma((1,)), dma((1,)),
            ],
            compiler_params=pltpu.CompilerParams(collective_id=0, has_side_effects=True, vmem_limit_bytes=60 * 1024 * 1024),
        )(ids, x_loc.reshape(tokens, hidden), r_loc.reshape(tokens, hidden), w_gate.T, w_in_loc[0], w_out_loc[0])
        loss, gx, gg, gw1, gw2 = out
        return loss[0, 0], gx.reshape(x_loc.shape), gw1[None], gw2[None], gg.T

    row_spec = P('ep', None, None)
    id_spec = P('ep', None)
    return jax.shard_map(layer_body, mesh=mesh, in_specs=(row_spec, row_spec, P(None, None), row_spec, row_spec, id_spec, id_spec, id_spec), out_specs=(P(), row_spec, row_spec, row_spec, P(None, None)), check_vma=False)
```

time: 285 us -> 97.2 us (0.34)
  waiting for transfers between devices: 152 us -> 0 us
  Pallas kernels: 0 us -> 82.4 us
  blocking collectives: 40.7 us -> 0 us
  matrix products: 40.4 us -> 0 us
  starting transfers between devices: 19.9 us -> 0 us
  between operations: 18 us -> 0.66 us
  local copies, waits for them, and re-layouts: 8.88 us -> 13.2 us
  other arithmetic: 4.84 us -> 0.67 us
    psum x1 -> x0, waiting for transfers between devices: 125 us -> none  [layer_body(): lax.psum(jnp.einsum('gsh,gse->he', x_loc, grad_logits_bf, preferred_eleme...]
    pallas_call x0 -> x1, Pallas kernels: none -> 82.4 us  [layer_body(): pl.pallas_call(functools.partial(layer_kernel, n, cap, seq), name='moe_la...]
    psum x1 -> x0, blocking collectives: 40.7 us -> none  [layer_body(): global_stats = lax.psum(local_stats, 'ep')]
    dot_general x16 -> x0, matrix products: 40.4 us -> none  [the longest x1 8.79 us: layer_body(): jnp.einsum('egch,efh->egcf', grad_y, w_out_loc, preferred_element_type=jn...]
    all_to_all x4 -> x0, waiting for transfers between devices: 27.3 us -> none  [the longest x1 17.3 us: layer_body(): expert_x = lax.all_to_all(send_x, 'ep', 0, 1, tiled=True)]
    all_to_all x4 -> x0, starting transfers between devices: 19.9 us -> none  [the longest x1 7.36 us: layer_body(): expert_x = lax.all_to_all(send_x, 'ep', 0, 1, tiled=True)]
    unnamed x25 -> x10, local copies, waits for them, and re-layouts: 1.61 us -> 9.66 us
    convert_element_type x4 -> x0, local copies, waits for them, and re-layouts: 6.02 us -> none  [the longest x1 1.55 us: layer_body(): jnp.einsum('egcf,efh->egch', act_bf, w_out_loc, preferred_element_type=jn...]
  transfers between devices with their start and end apart: 5 -> 0, of which waited for: 3 -> 0; matrix products, arithmetic and copies ran while one was open for 15% -> 0% of each run, Pallas kernels for 0% -> 0%
where the time goes in v2:
time: 97.2 us; the launch traced here: 97 us
  Pallas kernels  82.4 us (85%)
  local copies, waits for them, and re-layouts  13.2 us (14%)
    pallas_call x1, Pallas kernels, layer_body(): pl.pallas_call(functools.partial(layer_kernel, n, cap, seq), name='moe_la...  82.4 us
    unnamed x10, local copies, waits for them, and re-layouts  9.66 us

profile of v2, /device:TPU:0, one launch (start us, length us, event | category | flops | bytes accessed | tf_op | source)
XLA Modules:
  0.0 97.0 jit_solution(3951123539506384701)
XLA Ops:
  0.6 0.1 pad.3.clone
  0.7 0.8 reshape.28
  1.5 0.8 reshape.29
  2.2 0.8 reshape.30
  3.0 0.7 add_add_fusion.ids_ref
  3.7 82.4 %moe_layer.1 = (f32[8,128]{1,0:T(8,128)}, bf16[256,768]{1,0:T(8,128)(2,1)}, f32[32,768]{1,0:T(8,128)}, bf16[768,3072]{1,0:T(8,128)(2,1)}, bf16[3072,768]{1,0:T(8,128)(2,1)}) custom-call(s32[8,256]{1,0:T(8,128)} %add_add_fusion.ids_ref, bf16[256,768]{1,0:T(8,128)(2,1)} %bitcast.16, bf16[256,768]{1,0:T(8,128)(2,1)} %bitcast.17, bf16[32,768]{1,0:T(8,128)(2,1)} %bitcast.20, ...), custom_call_target="tpu_custom_call" | custom-call | tf_op jit(solution)/shard_map/moe_layer/pallas_call | solution.py:334
  86.1 1.2 %slice.3 = f32[1,1]{1,0:T(1,128)} slice(f32[8,128]{1,0:T(8,128)} %get-tuple-element.10), slice={[0:1], [0:1]} | slice | bytes 8 | tf_op jit(solution)/shard_map/slice | solution.py:377
  87.3 0.0 slice-start
  87.3 1.9 %copy.17 = bf16[4,64,768]{2,1,0:T(8,128)(2,1)} copy(bf16[4,64,768]{2,1,0:T(8,128)(2,1)} %bitcast.18) | data formatting | bytes 786432
  89.2 0.0 slice-start.1
  89.2 4.9 %copy.18 = bf16[1,768,3072]{2,1,0:T(8,128)(2,1)} copy(bf16[1,768,3072]{2,1,0:T(8,128)(2,1)} %bitcast.15) | data formatting | bytes 9437184
  94.1 0.0 slice-done
  94.1 0.0 slice-done.1
  94.1 0.0 copy-start
  94.1 2.2 %copy.19 = bf16[1,3072,768]{2,1,0:T(8,128)(2,1)} copy(bf16[1,3072,768]{2,1,0:T(8,128)(2,1)S(1)} %bitcast.14) | data formatting | bytes 9437184
  96.3 0.0 copy-done
  96.3 0.6 copy.20
  (2 shorter events, 0.0 us)
Async XLA Ops:
  87.3 6.8 %slice-start = ((s8[4718592]{0:T(1024)(128)(4,1)}), s8[4194304]{0:T(1024)(128)(4,1)S(1)}, s32[]{:S(2)}) async-start(s8[4718592]{0:T(1024)(128)(4,1)} %bitcast.12), calls=%async_computation | async-start | bytes 8388608
  89.2 4.9 %slice-start.1 = ((s8[4718592]{0:T(1024)(128)(4,1)}), s8[524288]{0:T(1024)(128)(4,1)S(1)}, s32[]{:S(2)}) async-start(s8[4718592]{0:T(1024)(128)(4,1)} %bitcast.12), calls=%async_computation.1 | async-start | bytes 1048576
  94.1 2.2 %copy-start = (f32[32,768]{1,0:T(8,128)S(1)}, f32[32,768]{1,0:T(8,128)}, u32[]{:S(2)}) copy-start(f32[32,768]{1,0:T(8,128)} %get-tuple-element.14) | copy-start | bytes 294916

commit v3 on v2

--- a/solution.py
+++ b/solution.py
@@ -30,11 +30,11 @@
     return a + b - 2 * a * b
 
 
-def layer_kernel(n, cap, seq, ids_ref, x_ref, r_ref, wg_ref, w1_hbm, w2_hbm,
-                 loss_ref, gx_ref, gg_ref, gw1_hbm, gw2_hbm,
+def layer_kernel(n, cap, seq, e1_ref, e2_ref, k2_ref, x_ref, r_ref, wg_ref, w1_hbm, w2_hbm,
+                 loss_ref, gx_ref, gg_ref, gw1, gw2,
                  w1, w2, sx, sr, xe, re, gy, act, gpre, gs, gback, rows_s, rows_r, dots_s, dots_r,
-                 part_s, part_r, sum_s, hacc, gacc, xet, stage1, stage2,
-                 w_sem, out_sem, s_x, s_r, s_g, s_row, s_dot, s_part, s_sum,
+                 part_s, part_r, sum_s, acc, slope, hid, xet,
+                 w_sem, s_x, s_r, s_g, s_row, s_dot, s_part, s_sum,
                  v_x, v_r, v_g, v_row, v_dot, v_part, v_sum):
     me = lax.axis_index('ep')
     tokens, hidden = x_ref.shape
@@ -79,7 +79,14 @@
     w1_copy.start()
     w2_copy.start()
 
-    e1, e2, k2 = ids_ref[0:1, :], ids_ref[1:2, :], ids_ref[2:3, :]
+    spread = (iota((seq, tokens), 1) % seq == iota((seq, tokens), 0)).astype(F32).astype(BF16)
+    own_group = iota((groups, tokens), 1) // seq == iota((groups, tokens), 0)
+
+    def along_lanes(ref):
+        wide = dot(ref[...].astype(F32).astype(BF16), spread)
+        return jnp.sum(jnp.where(own_group, wide, 0.0), axis=0, keepdims=True).astype(jnp.int32)
+
+    e1, e2, k2 = along_lanes(e1_ref), along_lanes(e2_ref), along_lanes(k2_ref)
     row_i, col_i = iota((tokens, tokens), 0), iota((tokens, tokens), 1)
     eye = row_i == col_i
 
@@ -112,6 +119,34 @@
     slot_i = iota((slots, tokens), 0)
     disp = ((slot_i == key1) | (slot_i == key2)).astype(F32).astype(BF16)
 
+    x = x_ref[...]
+    sx[...] = dot(disp, x).astype(BF16)
+
+    pl.semaphore_wait(barrier, n - 1)
+
+    def one_row(src, dst, src_row, send, recv, q, d):
+        return pltpu.make_async_remote_copy(src.at[pl.ds(src_row, 1)], dst.at[pl.ds(me, 1)], send.at[q], recv.at[0], device_id=(d,), device_id_type=MESH)
+
+    def block(src, dst, send, recv, half_i, q, d):
+        at = pl.ds(q * rows, rows)
+        return pltpu.make_async_remote_copy(src.at[at], dst.at[at], send.at[half_i], recv.at[half_i], device_id=(d,), device_id_type=MESH)
+
+    def own_row(src, dst, src_row, recv):
+        pltpu.make_async_copy(src.at[pl.ds(src_row, 1)], dst.at[pl.ds(me, 1)], recv.at[0]).start()
+
+    def own_block(src, dst, recv):
+        pltpu.make_async_copy(src.at[pl.ds(0, rows)], dst.at[pl.ds(0, rows)], recv.at[0]).start()
+
+    def settle(ref, sem, rows_at):
+        pltpu.make_async_copy(ref.at[rows_at], ref.at[rows_at], sem).wait()
+
+    def half_at(c):
+        return pl.ds(c * half, half)
+
+    for c in range(2):
+        each_partner(quarters_of[c], lambda q, d: block(sx, xe, s_x, v_x, c, q, d).start())
+    own_block(sx, xe, v_x)
+
     expert_i = iota((n, tokens), 0)
     hot1 = (expert_i == e1).astype(F32)
     hot2 = (expert_i == e2).astype(F32)
@@ -119,8 +154,6 @@
     at1 = (place_i == place1).astype(F32)
     at2 = (place_i == place2).astype(F32)
 
-    x = x_ref[...]
-    r = r_ref[...]
     wgt = wg_ref[...]
     logits = dot(wgt, x, NT)
     top_logit = jnp.max(logits, axis=0, keepdims=True)
@@ -140,56 +173,51 @@
     def as_column(row, base):
         return jnp.sum(jnp.where(lane_n == sub_n + base, row, 0.0), axis=1, keepdims=True)
 
+    r = r_ref[...]
     xr = jnp.sum(jnp.sum(x.astype(F32) * r.astype(F32), axis=0, keepdims=True), axis=1, keepdims=True)
     lane_1 = iota((1, 128), 1)
     stats = as_lanes(jnp.sum(hot1, axis=1, keepdims=True), 32) + as_lanes(jnp.sum(prob, axis=1, keepdims=True), 64) + jnp.where(lane_1 == 96, xr, 0.0)
     rows_s[...] = norm_rows + stats
 
-    sx[...] = dot(disp, x).astype(BF16)
     sr[...] = dot(disp, r).astype(BF16)
-
-    pl.semaphore_wait(barrier, n - 1)
-
-    def one_row(src, dst, src_row, send, recv, q, d):
-        return pltpu.make_async_remote_copy(src.at[pl.ds(src_row, 1)], dst.at[pl.ds(me, 1)], send.at[q], recv.at[0], device_id=(d,), device_id_type=MESH)
-
-    def block(src, dst, send, recv, half_i, q, d):
-        at = pl.ds(q * rows, rows)
-        return pltpu.make_async_remote_copy(src.at[at], dst.at[at], send.at[half_i], recv.at[half_i], device_id=(d,), device_id_type=MESH)
-
-    def own_row(src, dst, src_row, recv):
-        pltpu.make_async_copy(src.at[pl.ds(src_row, 1)], dst.at[pl.ds(me, 1)], recv.at[0]).start()
-
-    def own_block(src, dst, recv):
-        pltpu.make_async_copy(src.at[pl.ds(0, rows)], dst.at[pl.ds(0, rows)], recv.at[0]).start()
-
-    def settle(ref, sem, rows_at):
-        pltpu.make_async_copy(ref.at[rows_at], ref.at[rows_at], sem).wait()
-
-    def half_at(c):
-        return pl.ds(c * half, half)
-
     each_partner(everyone, lambda q, d: one_row(rows_s, rows_r, d, s_row, v_row, q, d).start())
     own_row(rows_s, rows_r, me, v_row)
-    own_block(sx, xe, v_x)
+    for c in range(2):
+        each_partner(quarters_of[c], lambda q, d: block(sr, re, s_r, v_r, c, q, d).start())
     own_block(sr, re, v_r)
-    for c in range(2):
-        each_partner(quarters_of[c], lambda q, d: block(sx, xe, s_x, v_x, c, q, d).start())
-        each_partner(quarters_of[c], lambda q, d: block(sr, re, s_r, v_r, c, q, d).start())
+
+    w1_copy.wait()
+    w2_copy.wait()
+    for c in range(2):
+        at = half_at(c)
+        settle(xe, v_x.at[c], at)
+        acc[...] = jnp.zeros_like(acc)
+
+        @pl.loop(0, tiles)
+        def _(f):
+            cols = pl.ds(pl.multiple_of(f * tile, tile), tile)
+            pre = dot(xe[at, :], w1[:, cols])
+            sq = pre * pre
+            th = jnp.tanh(GELU_C * (pre + GELU_K * (sq * pre)))
+            cdf = 0.5 * (1.0 + th)
+            a = (pre * cdf).astype(BF16)
+            slope[at, cols] = cdf + (0.5 * GELU_C) * pre * (1.0 - th * th) * (1.0 + 3 * GELU_K * sq)
+            act[at, cols] = a
+            acc[...] += dot(a, w2[cols, :])
+
+        hid[at, :] = acc[...].astype(BF16)
+
+    xet[...] = jnp.transpose(xe[...])
 
     settle(rows_r, v_row.at[0], pl.ds(0, n))
     all_rows = rows_r[...]
     total = jnp.sum(all_rows, axis=0, keepdims=True)
     frac = as_column(total, 32) / tokens_all
     mean_prob = as_column(total, 64) / tokens_all
-    w1_copy.wait()
-    w2_copy.wait()
 
     loss_part = jnp.zeros((1, 1), F32)
     for c in range(2):
         at = half_at(c)
-        settle(xe, v_x.at[c], at)
-        settle(re, v_r.at[c], at)
         slot_row = iota((half, n), 0) + c * half
         apart = slot_row // rows
         top = apart // plane
@@ -198,65 +226,36 @@
         wide = dot(pick, all_rows.astype(BF16))
         mine = iota((half, 128), 1) == iota((half, 128), 0) % rows
         norm = jnp.sum(jnp.where(mine, wide, 0.0), axis=1, keepdims=True)
-        xc = xe[at, :]
+        settle(re, v_r.at[c], at)
         rc = re[at, :].astype(F32)
         gy[at, :] = (norm * rc).astype(BF16)
-        hacc[...] = jnp.zeros_like(hacc)
-        gacc[...] = jnp.zeros_like(gacc)
-
-        @pl.loop(0, tiles)
-        def _(f):
-            cols = pl.ds(pl.multiple_of(f * tile, tile), tile)
-            w1t = w1[:, cols]
-            w2t = w2[cols, :]
-            pre = dot(xe[at, :], w1t)
-            sq = pre * pre
-            th = jnp.tanh(GELU_C * (pre + GELU_K * (sq * pre)))
-            cdf = 0.5 * (1.0 + th)
-            a = (pre * cdf).astype(BF16)
-            slope = cdf + (0.5 * GELU_C) * pre * (1.0 - th * th) * (1.0 + 3 * GELU_K * sq)
-            act[at, cols] = a
-            hacc[...] += dot(a, w2t)
-            ga = dot(gy[at, :], w2t, NT).astype(BF16)
-            gp = (ga.astype(F32) * slope).astype(BF16)
-            gpre[at, cols] = gp
-            gacc[...] += dot(gp, w1t, NT)
-
-        h = hacc[...].astype(BF16).astype(F32)
-        d = jnp.sum(h * rc, axis=1, keepdims=True)
+        d = jnp.sum(hid[at, :].astype(F32) * rc, axis=1, keepdims=True)
         loss_part = loss_part + jnp.sum(norm * d, axis=0, keepdims=True)
-        spread = jnp.where(mine, d, 0.0)
-        dots_s[pl.ds(c * (n // 2), n // 2), :] = jnp.sum(spread.reshape(n // 2, rows, 128), axis=1)
-        gs[at, :] = gacc[...].astype(BF16)
+        in_lane = jnp.where(mine, d, 0.0)
+        dots_s[pl.ds(c * (n // 2), n // 2), :] = jnp.sum(in_lane.reshape(n // 2, rows, 128), axis=1)
         if c == 1:
             dots_s[...] = dots_s[...] + jnp.where(lane_1 == 16, loss_part, 0.0)
             each_partner(everyone, lambda q, d: one_row(dots_s, dots_r, q, s_dot, v_dot, q, d).start())
             own_row(dots_s, dots_r, 0, v_dot)
-        else:
+        acc[...] = jnp.zeros_like(acc)
+
+        @pl.loop(0, tiles)
+        def _(f):
+            cols = pl.ds(pl.multiple_of(f * tile, tile), tile)
+            ga = dot(gy[at, :], w2[cols, :], NT).astype(BF16)
+            gp = (ga.astype(F32) * slope[at, cols]).astype(BF16)
+            gpre[at, cols] = gp
+            acc[...] += dot(gp, w1[:, cols], NT)
+
+        gs[at, :] = acc[...].astype(BF16)
+        if c == 0:
             own_block(gs, gback, v_g)
         each_partner(quarters_of[c], lambda q, d: block(gs, gback, s_g, v_g, c, q, d).start())
 
-    def put1(f, slot):
-        cols = pl.ds(pl.multiple_of(f * tile, tile), tile)
-        return pltpu.make_async_copy(stage1.at[slot], gw1_hbm.at[:, cols], out_sem.at[slot])
-
-    def put2(f, slot):
-        cols = pl.ds(pl.multiple_of(f * tile, tile), tile)
-        return pltpu.make_async_copy(stage2.at[slot], gw2_hbm.at[cols, :], out_sem.at[2 + slot])
-
-    xet[...] = jnp.transpose(xe[...])
-
     @pl.loop(0, tiles)
     def _(f):
-        slot = lax.rem(f, 2)
-
-        @pl.when(f >= 2)
-        def _():
-            put1(f - 2, slot).wait()
-
         cols = pl.ds(pl.multiple_of(f * tile, tile), tile)
-        stage1[slot] = dot(xet[...], gpre[:, cols]).astype(BF16)
-        put1(f, slot).start()
+        gw1[:, cols] = dot(xet[...], gpre[:, cols]).astype(BF16)
 
     settle(dots_r, v_dot.at[0], pl.ds(0, n))
     all_dots = dots_r[...]
@@ -281,15 +280,8 @@
 
     @pl.loop(0, tiles)
     def _(f):
-        slot = lax.rem(f, 2)
-
-        @pl.when(f >= 2)
-        def _():
-            put2(f - 2, slot).wait()
-
         cols = pl.ds(pl.multiple_of(f * tile, tile), tile)
-        stage2[slot] = dot(act[:, cols], gy[...], TN).astype(BF16)
-        put2(f, slot).start()
+        gw2[cols, :] = dot(act[:, cols], gy[...], TN).astype(BF16)
 
     settle(part_r, v_part.at[0], pl.ds(0, n))
     sum_s[0:1, :] = jnp.sum(part_r[...], axis=0, keepdims=True)
@@ -305,9 +297,6 @@
     gx_ref[...] = (near + dot(comb, gback[...])).astype(BF16)
 
     settle(gg_ref, v_sum.at[0], pl.ds(0, n))
-    for f in range(tiles - 2, tiles):
-        put1(f, f % 2).wait()
-        put2(f, f % 2).wait()
     each_partner(everyone, lambda q, d: one_row(rows_s, rows_r, d, s_row, v_row, q, d).wait_send())
     each_partner(everyone, lambda q, d: one_row(dots_s, dots_r, q, s_dot, v_dot, q, d).wait_send())
     each_partner(everyone, lambda q, d: one_row(part_s, part_r, d, s_part, v_part, q, d).wait_send())
@@ -326,8 +315,6 @@
         ff = w_in_loc.shape[2]
         tokens = groups * seq
         slots = n * groups * cap
-        tile = 512
-        ids = jnp.concatenate([first_ids.reshape(1, tokens), second_ids.reshape(1, tokens), keep_ids.reshape(1, tokens), jnp.zeros((5, tokens), jnp.int32)])
         vmem = pl.BlockSpec(memory_space=pltpu.VMEM)
         hbm = pl.BlockSpec(memory_space=pl.ANY)
         dma = pltpu.SemaphoreType.DMA
@@ -335,14 +322,14 @@
             functools.partial(layer_kernel, n, cap, seq),
             name='moe_layer',
             out_shape=(
-                jax.ShapeDtypeStruct((8, 128), F32),
-                jax.ShapeDtypeStruct((tokens, hidden), BF16),
-                jax.ShapeDtypeStruct((n, hidden), F32),
-                jax.ShapeDtypeStruct((hidden, ff), BF16),
-                jax.ShapeDtypeStruct((ff, hidden), BF16),
+                pltpu.VMEM((8, 128), F32),
+                pltpu.VMEM((tokens, hidden), BF16),
+                pltpu.VMEM((n, hidden), F32),
+                pltpu.VMEM((hidden, ff), BF16),
+                pltpu.VMEM((ff, hidden), BF16),
             ),
-            in_specs=[vmem, vmem, vmem, vmem, hbm, hbm],
-            out_specs=(vmem, vmem, vmem, hbm, hbm),
+            in_specs=[vmem] * 6 + [hbm, hbm],
+            out_specs=(vmem,) * 5,
             scratch_shapes=[
                 pltpu.VMEM((hidden, ff), BF16),
                 pltpu.VMEM((ff, hidden), BF16),
@@ -363,16 +350,15 @@
                 pltpu.VMEM((n, hidden), F32),
                 pltpu.VMEM((8, hidden), F32),
                 pltpu.VMEM((slots // 2, hidden), F32),
-                pltpu.VMEM((slots // 2, hidden), F32),
+                pltpu.VMEM((slots, ff), F32),
+                pltpu.VMEM((slots, hidden), BF16),
                 pltpu.VMEM((hidden, slots), BF16),
-                pltpu.VMEM((2, hidden, tile), BF16),
-                pltpu.VMEM((2, tile, hidden), BF16),
-                dma((2,)), dma((4,)),
+                dma((2,)),
                 dma((2,)), dma((2,)), dma((2,)), dma((n,)), dma((n,)), dma((n,)), dma((n,)),
                 dma((2,)), dma((2,)), dma((2,)), dma((1,)), dma((1,)), dma((1,)), dma((1,)),
             ],
-            compiler_params=pltpu.CompilerParams(collective_id=0, has_side_effects=True, vmem_limit_bytes=60 * 1024 * 1024),
-        )(ids, x_loc.reshape(tokens, hidden), r_loc.reshape(tokens, hidden), w_gate.T, w_in_loc[0], w_out_loc[0])
+            compiler_params=pltpu.CompilerParams(collective_id=0, has_side_effects=True, vmem_limit_bytes=44 * 1024 * 1024),
+        )(first_ids, second_ids, keep_ids, x_loc.reshape(tokens, hidden), r_loc.reshape(tokens, hidden), w_gate.T, w_in_loc[0], w_out_loc[0])
         loss, gx, gg, gw1, gw2 = out
         return loss[0, 0], gx.reshape(x_loc.shape), gw1[None], gw2[None], gg.T
 

time: 97.2 us -> 85.1 us (0.88)
  Pallas kernels: 82.4 us -> 74.1 us
  local copies, waits for them, and re-layouts: 13.2 us -> 10.1 us
    pallas_call x1, Pallas kernels: 82.4 us -> 74.1 us  [layer_body(): pl.pallas_call(functools.partial(layer_kernel, n, cap, seq), name='moe_la...]
    reshape x3 -> x0, local copies, waits for them, and re-layouts: 2.28 us -> none  [the longest x1 0.76 us: layer_body(): first_ids.reshape(1, tokens)]
    unnamed x10 -> x14, local copies, waits for them, and re-layouts: 9.66 us -> 9.59 us
where the time goes in v3:
time: 85.1 us; the launch traced here: 84.8 us
  Pallas kernels  74.1 us (87%)
  local copies, waits for them, and re-layouts  10.1 us (12%)
    pallas_call x1, Pallas kernels, layer_body(): pl.pallas_call(functools.partial(layer_kernel, n, cap, seq), name='moe_la...  74.1 us
    unnamed x14, local copies, waits for them, and re-layouts  9.59 us

profile of v3, /device:TPU:0, one launch (start us, length us, event | category | flops | bytes accessed | tf_op | source)
XLA Modules:
  0.0 84.8 jit_solution(16600554728395577816)
XLA Ops:
  0.6 0.0 copy-start
  0.6 1.0 %copy-done = bf16[4,64,768]{2,1,0:T(8,128)(2,1)S(1)} copy-done((bf16[4,64,768]{2,1,0:T(8,128)(2,1)S(1)}, bf16[4,64,768]{2,1,0:T(8,128)(2,1)}, u32[]{:S(2)}) %copy-start) | copy-done | bytes 393240
  1.6 0.0 copy-start.1
  1.6 0.8 copy-done.1
  2.4 0.0 copy-start.2
  2.4 0.7 copy-done.2
  3.1 0.0 copy-start.3
  3.1 0.7 copy-done.3
  3.8 0.0 copy-start.4
  3.8 0.7 copy-done.4
  4.5 74.1 %moe_layer.1 = (f32[8,128]{1,0:T(8,128)S(1)}, bf16[256,768]{1,0:T(8,128)(2,1)S(1)}, f32[32,768]{1,0:T(8,128)S(1)}, bf16[768,3072]{1,0:T(8,128)(2,1)S(1)}, bf16[3072,768]{1,0:T(8,128)(2,1)S(1)}) custom-call(s32[4,64]{1,0:T(4,128)S(1)} %copy-done.2, s32[4,64]{1,0:T(4,128)S(1)} %copy-done.3, s32[4,64]{1,0:T(4,128)S(1)} %copy-done.4, ...), custom_call_target="tpu_custom_call" | custom-call | tf_op jit(solution)/shard_map/moe_layer/pallas_call | solution.py:321
  78.5 0.5 slice.3
  79.1 0.7 copy.17
  79.8 0.6 copy.20
  80.4 2.2 %copy.18 = bf16[1,768,3072]{2,1,0:T(8,128)(2,1)} copy(bf16[1,768,3072]{2,1,0:T(8,128)(2,1)S(1)} %bitcast.11) | data formatting | bytes 9437184
  82.6 2.2 %copy.19 = bf16[1,3072,768]{2,1,0:T(8,128)(2,1)} copy(bf16[1,3072,768]{2,1,0:T(8,128)(2,1)S(1)} %bitcast.10) | data formatting | bytes 9437184
Async XLA Ops:
  0.6 1.0 %copy-start = (bf16[4,64,768]{2,1,0:T(8,128)(2,1)S(1)}, bf16[4,64,768]{2,1,0:T(8,128)(2,1)}, u32[]{:S(2)}) copy-start(bf16[4,64,768]{2,1,0:T(8,128)(2,1)} %param.8) | copy-start | bytes 1179652
  1.6 0.8 copy-start.1
  2.4 0.7 copy-start.2
  3.1 0.7 copy-start.3
  3.8 0.7 copy-start.4

commit v4 on v3

--- a/solution.py
+++ b/solution.py
@@ -30,11 +30,20 @@
     return a + b - 2 * a * b
 
 
-def layer_kernel(n, cap, seq, e1_ref, e2_ref, k2_ref, x_ref, r_ref, wg_ref, w1_hbm, w2_hbm,
+def write_kernel(loss_v, gx_v, gg_v, gw1_v, gw2_v, loss_s, gx_h, gg_h, gw1_h, gw2_h, sem):
+    copies = [pltpu.make_async_copy(src, dst, sem.at[i]) for i, (src, dst) in enumerate(((gw1_v, gw1_h), (gw2_v, gw2_h), (gx_v, gx_h), (gg_v, gg_h)))]
+    for copy in copies:
+        copy.start()
+    loss_s[0, 0] = jnp.max(loss_v[...])
+    for copy in copies:
+        copy.wait()
+
+
+def layer_kernel(n, cap, seq, e1_hbm, e2_hbm, k2_hbm, x_hbm, r_hbm, wg_hbm, w1_hbm, w2_hbm,
                  loss_ref, gx_ref, gg_ref, gw1, gw2,
-                 w1, w2, sx, sr, xe, re, gy, act, gpre, gs, gback, rows_s, rows_r, dots_s, dots_r,
-                 part_s, part_r, sum_s, acc, slope, hid, xet,
-                 w_sem, s_x, s_r, s_g, s_row, s_dot, s_part, s_sum,
+                 e1_ref, e2_ref, k2_ref, x_ref, r_ref, wg_ref, w1, w2, sx, sr, xe, re, gy, act, gpre, gs, gback,
+                 rows_s, rows_r, dots_s, dots_r, part_s, part_r, sum_s, acc, slope, hid, xet, in_sem,
+                 s_x, s_r, s_g, s_row, s_dot, s_part, s_sum,
                  v_x, v_r, v_g, v_row, v_dot, v_part, v_sum):
     me = lax.axis_index('ep')
     tokens, hidden = x_ref.shape
@@ -42,7 +51,6 @@
     groups = tokens // seq
     rows = groups * cap
     slots = n * rows
-    half = slots // 2
     plane = n // 4
     tokens_all = tokens * n
     numel = tokens_all * hidden
@@ -52,7 +60,8 @@
     low, high = lax.rem(me, plane), lax.div(me, plane)
     low_bits = [lax.rem(low, 2), lax.rem(lax.div(low, 2), 2), lax.div(low, 4)]
     high_bits = [lax.rem(high, 2), lax.div(high, 2)]
-    order = (0, 2, 1, 3)
+    order = (2, 0, 1, 3)
+    own = plane * rows
 
     def partner(quarter, step):
         far = order[quarter]
@@ -61,23 +70,27 @@
         bits = [flip_bits(a, b) for a, b in zip(low_bits, step_bits)]
         return (top[0] + 2 * top[1]) * plane + bits[0] + 2 * bits[1] + 4 * bits[2]
 
-    def each_partner(quarters, body):
-        for quarter in quarters:
-            first = 1 if quarter == 0 else 0
-
-            @pl.loop(first, plane)
+    def each_partner(pieces, body):
+        for quarter, lo, hi in pieces:
+            first = max(lo, 1) if order[quarter] == 0 else lo
+
+            @pl.loop(first, hi)
             def _(step):
                 body(quarter * plane + step, partner(quarter, step))
 
-    everyone = (0, 1, 2, 3)
-    quarters_of = ((0, 1), (2, 3))
+    everyone = tuple((quarter, 0, plane) for quarter in (0, 3, 1, 2))
+    early, near, late = 0, 1, 2
+    quarters_of = (((0, 0, plane),), ((1, 0, plane), (2, 0, plane)), ((3, 0, plane),))
+    span = ((0, plane * rows), (plane * rows, 2 * plane * rows), (3 * plane * rows, plane * rows))
 
     barrier = pltpu.get_barrier_semaphore()
     each_partner(everyone, lambda q, d: pl.semaphore_signal(barrier, inc=1, device_id=(d,), device_id_type=MESH))
-    w1_copy = pltpu.make_async_copy(w1_hbm, w1, w_sem.at[0])
-    w2_copy = pltpu.make_async_copy(w2_hbm, w2, w_sem.at[1])
-    w1_copy.start()
-    w2_copy.start()
+    fetched = [pltpu.make_async_copy(src, dst, in_sem.at[i]) for i, (src, dst) in enumerate((
+        (e1_hbm, e1_ref), (e2_hbm, e2_ref), (k2_hbm, k2_ref), (x_hbm, x_ref), (r_hbm, r_ref), (wg_hbm, wg_ref), (w1_hbm, w1), (w2_hbm, w2)))]
+    for copy in fetched:
+        copy.start()
+    for copy in fetched[:3]:
+        copy.wait()
 
     spread = (iota((seq, tokens), 1) % seq == iota((seq, tokens), 0)).astype(F32).astype(BF16)
     own_group = iota((groups, tokens), 1) // seq == iota((groups, tokens), 0)
@@ -111,14 +124,15 @@
     def slot_of(expert):
         apart = expert ^ me
         top = apart // plane
-        swapped = (top // 2) + 2 * (top % 2)
-        return swapped * plane + apart % plane
+        quarter = jnp.where(top == order[0], 0, jnp.where(top == order[3], 3, top + 1))
+        return quarter * plane + apart % plane
 
     key1 = jnp.where(kept1, slot_of(e1) * rows + place1, -1)
     key2 = jnp.where(kept2, slot_of(e2) * rows + place2, -1)
     slot_i = iota((slots, tokens), 0)
     disp = ((slot_i == key1) | (slot_i == key2)).astype(F32).astype(BF16)
 
+    fetched[3].wait()
     x = x_ref[...]
     sx[...] = dot(disp, x).astype(BF16)
 
@@ -135,17 +149,22 @@
         pltpu.make_async_copy(src.at[pl.ds(src_row, 1)], dst.at[pl.ds(me, 1)], recv.at[0]).start()
 
     def own_block(src, dst, recv):
-        pltpu.make_async_copy(src.at[pl.ds(0, rows)], dst.at[pl.ds(0, rows)], recv.at[0]).start()
+        pltpu.make_async_copy(src.at[pl.ds(own, rows)], dst.at[pl.ds(own, rows)], recv.at[near]).start()
 
     def settle(ref, sem, rows_at):
         pltpu.make_async_copy(ref.at[rows_at], ref.at[rows_at], sem).wait()
 
-    def half_at(c):
-        return pl.ds(c * half, half)
-
-    for c in range(2):
-        each_partner(quarters_of[c], lambda q, d: block(sx, xe, s_x, v_x, c, q, d).start())
+    def group_at(c):
+        return pl.ds(*span[c])
+
+    def send_group(src, dst, send, recv, c, pieces=None):
+        each_partner(pieces or quarters_of[c], lambda q, d: block(src, dst, send, recv, c, q, d).start())
+
+    send_group(sx, xe, s_x, v_x, early)
+    send_group(sx, xe, s_x, v_x, near)
     own_block(sx, xe, v_x)
+    fetched[4].wait()
+    fetched[5].wait()
 
     expert_i = iota((n, tokens), 0)
     hot1 = (expert_i == e1).astype(F32)
@@ -182,16 +201,29 @@
     sr[...] = dot(disp, r).astype(BF16)
     each_partner(everyone, lambda q, d: one_row(rows_s, rows_r, d, s_row, v_row, q, d).start())
     own_row(rows_s, rows_r, me, v_row)
-    for c in range(2):
-        each_partner(quarters_of[c], lambda q, d: block(sr, re, s_r, v_r, c, q, d).start())
+    send_group(sr, re, s_r, v_r, early)
+    send_group(sx, xe, s_x, v_x, late)
+    send_group(sr, re, s_r, v_r, near)
     own_block(sr, re, v_r)
-
-    w1_copy.wait()
-    w2_copy.wait()
-    for c in range(2):
-        at = half_at(c)
+    send_group(sr, re, s_r, v_r, late)
+
+    slot_row = iota((slots, n), 0)
+    quarter = slot_row // rows // plane
+    far = jnp.where(quarter == 0, order[0], jnp.where(quarter == 3, order[3], quarter - 1))
+    source = (far * plane + slot_row // rows % plane) ^ me
+    pick = (source == iota((slots, n), 1)).astype(F32).astype(BF16)
+    mine = iota((slots, 128), 1) == iota((slots, 128), 0) % rows
+    key1c, key2c = column(key1), column(key2)
+    slot_l = iota((tokens, slots), 1)
+    comb = ((slot_l == key1c) | (slot_l == key2c)).astype(F32).astype(BF16)
+    fetched[6].wait()
+    fetched[7].wait()
+
+    def forward(c):
+        at = group_at(c)
         settle(xe, v_x.at[c], at)
-        acc[...] = jnp.zeros_like(acc)
+        total_at = pl.ds(0, span[c][1])
+        acc[total_at, :] = jnp.zeros((span[c][1], hidden), F32)
 
         @pl.loop(0, tiles)
         def _(f):
@@ -203,41 +235,26 @@
             a = (pre * cdf).astype(BF16)
             slope[at, cols] = cdf + (0.5 * GELU_C) * pre * (1.0 - th * th) * (1.0 + 3 * GELU_K * sq)
             act[at, cols] = a
-            acc[...] += dot(a, w2[cols, :])
-
-        hid[at, :] = acc[...].astype(BF16)
-
-    xet[...] = jnp.transpose(xe[...])
-
-    settle(rows_r, v_row.at[0], pl.ds(0, n))
-    all_rows = rows_r[...]
-    total = jnp.sum(all_rows, axis=0, keepdims=True)
-    frac = as_column(total, 32) / tokens_all
-    mean_prob = as_column(total, 64) / tokens_all
-
-    loss_part = jnp.zeros((1, 1), F32)
-    for c in range(2):
-        at = half_at(c)
-        slot_row = iota((half, n), 0) + c * half
-        apart = slot_row // rows
-        top = apart // plane
-        source = (((top // 2) + 2 * (top % 2)) * plane + apart % plane) ^ me
-        pick = (source == iota((half, n), 1)).astype(F32).astype(BF16)
-        wide = dot(pick, all_rows.astype(BF16))
-        mine = iota((half, 128), 1) == iota((half, 128), 0) % rows
-        norm = jnp.sum(jnp.where(mine, wide, 0.0), axis=1, keepdims=True)
+            acc[total_at, :] += dot(a, w2[cols, :])
+
+        hid[at, :] = acc[total_at, :].astype(BF16)
+
+    def receive(c):
+        at = group_at(c)
+        start, size = span[c]
         settle(re, v_r.at[c], at)
         rc = re[at, :].astype(F32)
+        norm = norms[start:start + size]
         gy[at, :] = (norm * rc).astype(BF16)
         d = jnp.sum(hid[at, :].astype(F32) * rc, axis=1, keepdims=True)
-        loss_part = loss_part + jnp.sum(norm * d, axis=0, keepdims=True)
-        in_lane = jnp.where(mine, d, 0.0)
-        dots_s[pl.ds(c * (n // 2), n // 2), :] = jnp.sum(in_lane.reshape(n // 2, rows, 128), axis=1)
-        if c == 1:
-            dots_s[...] = dots_s[...] + jnp.where(lane_1 == 16, loss_part, 0.0)
-            each_partner(everyone, lambda q, d: one_row(dots_s, dots_r, q, s_dot, v_dot, q, d).start())
-            own_row(dots_s, dots_r, 0, v_dot)
-        acc[...] = jnp.zeros_like(acc)
+        in_lane = jnp.where(mine[start:start + size], d, 0.0)
+        dots_s[pl.ds(start // rows, size // rows), :] = jnp.sum(in_lane.reshape(size // rows, rows, 128), axis=1)
+        return jnp.sum(norm * d, axis=0, keepdims=True)
+
+    def backward(c):
+        at = group_at(c)
+        total_at = pl.ds(0, span[c][1])
+        acc[total_at, :] = jnp.zeros((span[c][1], hidden), F32)
 
         @pl.loop(0, tiles)
         def _(f):
@@ -245,17 +262,52 @@
             ga = dot(gy[at, :], w2[cols, :], NT).astype(BF16)
             gp = (ga.astype(F32) * slope[at, cols]).astype(BF16)
             gpre[at, cols] = gp
-            acc[...] += dot(gp, w1[:, cols], NT)
-
-        gs[at, :] = acc[...].astype(BF16)
-        if c == 0:
-            own_block(gs, gback, v_g)
-        each_partner(quarters_of[c], lambda q, d: block(gs, gback, s_g, v_g, c, q, d).start())
-
-    @pl.loop(0, tiles)
-    def _(f):
-        cols = pl.ds(pl.multiple_of(f * tile, tile), tile)
-        gw1[:, cols] = dot(xet[...], gpre[:, cols]).astype(BF16)
+            acc[total_at, :] += dot(gp, w1[:, cols], NT)
+
+        gs[at, :] = acc[total_at, :].astype(BF16)
+
+    def send_back(c, pieces=None):
+        send_group(gs, gback, s_g, v_g, c, pieces)
+
+    def grad_first(lo, hi):
+        @pl.loop(lo, hi)
+        def _(f):
+            cols = pl.ds(pl.multiple_of(f * tile, tile), tile)
+            gw1[:, cols] = dot(xet[...], gpre[:, cols]).astype(BF16)
+
+    def grad_second(lo, hi):
+        @pl.loop(lo, hi)
+        def _(f):
+            cols = pl.ds(pl.multiple_of(f * tile, tile), tile)
+            gw2[cols, :] = dot(act[:, cols], gy[...], TN).astype(BF16)
+
+    forward(early)
+    forward(near)
+    settle(rows_r, v_row.at[0], pl.ds(0, n))
+    all_rows = rows_r[...]
+    total = jnp.sum(all_rows, axis=0, keepdims=True)
+    frac = as_column(total, 32) / tokens_all
+    mean_prob = as_column(total, 64) / tokens_all
+    norms = jnp.sum(jnp.where(mine, dot(pick, all_rows.astype(BF16)), 0.0), axis=1, keepdims=True)
+
+    loss_part = receive(early)
+    backward(early)
+    split_early, split_late = 5, 2
+    send_back(early, ((0, 0, split_early),))
+    loss_part = loss_part + receive(near)
+    backward(near)
+    send_back(near)
+    own_block(gs, gback, v_g)
+    forward(late)
+    xet[...] = jnp.transpose(xe[...])
+    loss_part = loss_part + receive(late)
+    dots_s[...] = dots_s[...] + jnp.where(lane_1 == 16, loss_part, 0.0)
+    each_partner(everyone, lambda q, d: one_row(dots_s, dots_r, q, s_dot, v_dot, q, d).start())
+    own_row(dots_s, dots_r, plane, v_dot)
+    send_back(early, ((0, split_early, plane),))
+    backward(late)
+    send_back(late, ((3, 0, split_late),))
+    grad_first(0, 2)
 
     settle(dots_r, v_dot.at[0], pl.ds(0, n))
     all_dots = dots_r[...]
@@ -269,32 +321,31 @@
     up2 = (d2 - d1) * g1 / gate_sq
     gprob = up1 * hot1 + up2 * hot2 + (ALPHA * hidden * n) * frac
     glog = (prob * (gprob - jnp.sum(prob * gprob, axis=0, keepdims=True))).astype(BF16)
-    part_s[...] = dot(glog, x)
+    part_s[...] = dot(glog, x_ref[...])
     each_partner(everyone, lambda q, d: one_row(part_s, part_r, d, s_part, v_part, q, d).start())
     own_row(part_s, part_r, me, v_part)
+    send_back(late, ((3, split_late, plane),))
+    grad_first(2, tiles)
 
     both = jnp.sum(jnp.where(lane_1 == 96, total, 0.0), axis=1, keepdims=True)
     both = both + jnp.sum(jnp.where(lane_1 == 16, jnp.sum(all_dots, axis=0, keepdims=True), 0.0), axis=1, keepdims=True)
     aux = jnp.sum(frac * mean_prob, axis=0, keepdims=True) * n
     loss_ref[...] = jnp.broadcast_to(both / numel + ALPHA * aux, loss_ref.shape)
-
-    @pl.loop(0, tiles)
-    def _(f):
-        cols = pl.ds(pl.multiple_of(f * tile, tile), tile)
-        gw2[cols, :] = dot(act[:, cols], gy[...], TN).astype(BF16)
+    grad_second(0, 2)
 
     settle(part_r, v_part.at[0], pl.ds(0, n))
     sum_s[0:1, :] = jnp.sum(part_r[...], axis=0, keepdims=True)
     each_partner(everyone, lambda q, d: one_row(sum_s, gg_ref, 0, s_sum, v_sum, q, d).start())
     own_row(sum_s, gg_ref, 0, v_sum)
 
-    key1c, key2c = column(key1), column(key2)
-    slot_l = iota((tokens, slots), 1)
-    comb = ((slot_l == key1c) | (slot_l == key2c)).astype(F32).astype(BF16)
-    near = r.astype(F32) + dot(glog, wgt, TN)
-    for c in range(2):
-        settle(gback, v_g.at[c], half_at(c))
-    gx_ref[...] = (near + dot(comb, gback[...])).astype(BF16)
+    grad_second(2, tiles)
+
+    out = r_ref[...].astype(F32) + dot(glog, wg_ref[...], TN)
+    for c in (near, early, late):
+        start, size = span[c]
+        settle(gback, v_g.at[c], group_at(c))
+        out = out + dot(comb[:, start:start + size], gback[group_at(c), :])
+    gx_ref[...] = out.astype(BF16)
 
     settle(gg_ref, v_sum.at[0], pl.ds(0, n))
     each_partner(everyone, lambda q, d: one_row(rows_s, rows_r, d, s_row, v_row, q, d).wait_send())
@@ -302,8 +353,9 @@
     each_partner(everyone, lambda q, d: one_row(part_s, part_r, d, s_part, v_part, q, d).wait_send())
     each_partner(everyone, lambda q, d: one_row(sum_s, gg_ref, 0, s_sum, v_sum, q, d).wait_send())
     for ref, sem in ((sx, s_x), (sr, s_r), (gs, s_g)):
-        settle(ref, sem.at[0], pl.ds(rows, half - rows))
-        settle(ref, sem.at[1], half_at(1))
+        settle(ref, sem.at[early], group_at(early))
+        settle(ref, sem.at[near], pl.ds(own + rows, span[near][1] - rows))
+        settle(ref, sem.at[late], group_at(late))
 
 
 def solution(mesh):
@@ -316,7 +368,7 @@
         tokens = groups * seq
         slots = n * groups * cap
         vmem = pl.BlockSpec(memory_space=pltpu.VMEM)
-        hbm = pl.BlockSpec(memory_space=pl.ANY)
+        hbm = pl.BlockSpec(memory_space=pltpu.HBM)
         dma = pltpu.SemaphoreType.DMA
         out = pl.pallas_call(
             functools.partial(layer_kernel, n, cap, seq),
@@ -328,9 +380,15 @@
                 pltpu.VMEM((hidden, ff), BF16),
                 pltpu.VMEM((ff, hidden), BF16),
             ),
-            in_specs=[vmem] * 6 + [hbm, hbm],
+            in_specs=[hbm] * 8,
             out_specs=(vmem,) * 5,
             scratch_shapes=[
+                pltpu.VMEM((groups, seq), jnp.int32),
+                pltpu.VMEM((groups, seq), jnp.int32),
+                pltpu.VMEM((groups, seq), jnp.int32),
+                pltpu.VMEM((tokens, hidden), BF16),
+                pltpu.VMEM((tokens, hidden), BF16),
+                pltpu.VMEM((n, hidden), BF16),
                 pltpu.VMEM((hidden, ff), BF16),
                 pltpu.VMEM((ff, hidden), BF16),
                 pltpu.VMEM((slots, hidden), BF16),
@@ -353,14 +411,29 @@
                 pltpu.VMEM((slots, ff), F32),
                 pltpu.VMEM((slots, hidden), BF16),
                 pltpu.VMEM((hidden, slots), BF16),
-                dma((2,)),
-                dma((2,)), dma((2,)), dma((2,)), dma((n,)), dma((n,)), dma((n,)), dma((n,)),
-                dma((2,)), dma((2,)), dma((2,)), dma((1,)), dma((1,)), dma((1,)), dma((1,)),
+                dma((8,)),
+                dma((3,)), dma((3,)), dma((3,)), dma((n,)), dma((n,)), dma((n,)), dma((n,)),
+                dma((3,)), dma((3,)), dma((3,)), dma((1,)), dma((1,)), dma((1,)), dma((1,)),
             ],
             compiler_params=pltpu.CompilerParams(collective_id=0, has_side_effects=True, vmem_limit_bytes=44 * 1024 * 1024),
-        )(first_ids, second_ids, keep_ids, x_loc.reshape(tokens, hidden), r_loc.reshape(tokens, hidden), w_gate.T, w_in_loc[0], w_out_loc[0])
-        loss, gx, gg, gw1, gw2 = out
-        return loss[0, 0], gx.reshape(x_loc.shape), gw1[None], gw2[None], gg.T
+        )(*(pltpu.with_memory_space_constraint(a, pltpu.HBM) for a in (
+            first_ids, second_ids, keep_ids, x_loc.reshape(tokens, hidden), r_loc.reshape(tokens, hidden), w_gate.T, w_in_loc[0], w_out_loc[0])))
+        loss, gx, gg, gw1, gw2 = pl.pallas_call(
+            write_kernel,
+            name='write_results',
+            out_shape=(
+                jax.ShapeDtypeStruct((1, 1), F32),
+                jax.ShapeDtypeStruct((tokens, hidden), BF16),
+                jax.ShapeDtypeStruct((n, hidden), F32),
+                jax.ShapeDtypeStruct((hidden, ff), BF16),
+                jax.ShapeDtypeStruct((ff, hidden), BF16),
+            ),
+            in_specs=[vmem] * 5,
+            out_specs=(pl.BlockSpec(memory_space=pltpu.SMEM), hbm, hbm, hbm, hbm),
+            scratch_shapes=[dma((4,))],
+            compiler_params=pltpu.CompilerParams(vmem_limit_bytes=2 * 1024 * 1024),
+        )(*(pltpu.with_memory_space_constraint(a, pltpu.VMEM) for a in out))
+        return loss.reshape(()), gx.reshape(x_loc.shape), gw1[None], gw2[None], gg.T
 
     row_spec = P('ep', None, None)
     id_spec = P('ep', None)

time: 85.1 us -> 77.6 us (0.912)
  local copies, waits for them, and re-layouts: 10.1 us -> 0 us
  Pallas kernels: 74.1 us -> 76.8 us
    unnamed x14 -> x0, local copies, waits for them, and re-layouts: 9.59 us -> none
    pallas_call x0 -> x1, Pallas kernels: none -> 4.3 us  [layer_body(): pl.pallas_call(write_kernel, name='write_results', out_shape=(jax.ShapeDt...]
    pallas_call x1, Pallas kernels: 74.1 us -> 72.5 us  [layer_body(): pl.pallas_call(functools.partial(layer_kernel, n, cap, seq), name='moe_la...]
where the time goes in v4:
time: 77.6 us; the launch traced here: 77.4 us
  Pallas kernels  76.8 us (99%)
    pallas_call x1, Pallas kernels, layer_body(): pl.pallas_call(functools.partial(layer_kernel, n, cap, seq), name='moe_la...  72.5 us
    pallas_call x1, Pallas kernels, layer_body(): pl.pallas_call(write_kernel, name='write_results', out_shape=(jax.ShapeDt...  4.3 us

profile of v4, /device:TPU:0, one launch (start us, length us, event | category | flops | bytes accessed | tf_op | source)
XLA Modules:
  0.0 77.4 jit_solution(5063917717218258459)
XLA Ops:
  0.6 72.5 %moe_layer.1 = (f32[8,128]{1,0:T(8,128)S(1)}, bf16[256,768]{1,0:T(8,128)(2,1)S(1)}, f32[32,768]{1,0:T(8,128)S(1)}, bf16[768,3072]{1,0:T(8,128)(2,1)S(1)}, bf16[3072,768]{1,0:T(8,128)(2,1)S(1)}) custom-call(s32[4,64]{1,0:T(4,128)} %e1_hbm.1, s32[4,64]{1,0:T(4,128)} %e2_hbm.1, s32[4,64]{1,0:T(4,128)} %k2_hbm.1, bf16[256,768]{1,0:T(8,128)(2,1)} %bitcast.12, ...), custom_call_target="tpu_custom_call" | custom-call | tf_op jit(solution)/shard_map/moe_layer/pallas_call | solution.py:373
  73.1 4.3 %write_results.1 = (f32[1,1]{1,0:T(1,128)}, bf16[256,768]{1,0:T(8,128)(2,1)}, f32[32,768]{1,0:T(8,128)}, bf16[768,3072]{1,0:T(8,128)(2,1)}, bf16[3072,768]{1,0:T(8,128)(2,1)}) custom-call(f32[8,128]{1,0:T(8,128)S(1)} %get-tuple-element.15.loss_v, bf16[256,768]{1,0:T(8,128)(2,1)S(1)} %get-tuple-element.16.gx_v, f32[32,768]{1,0:T(8,128)S(1)} %get-tuple-element.17.gg_v, ...), custom_call_target="tpu_custom_call" | custom-call | tf_op jit(solution)/shard_map/write_results/pallas_call | solution.py:421

commit v5 on v4

--- a/solution.py
+++ b/solution.py
@@ -42,9 +42,9 @@
 def layer_kernel(n, cap, seq, e1_hbm, e2_hbm, k2_hbm, x_hbm, r_hbm, wg_hbm, w1_hbm, w2_hbm,
                  loss_ref, gx_ref, gg_ref, gw1, gw2,
                  e1_ref, e2_ref, k2_ref, x_ref, r_ref, wg_ref, w1, w2, sx, sr, xe, re, gy, act, gpre, gs, gback,
-                 rows_s, rows_r, dots_s, dots_r, part_s, part_r, sum_s, acc, slope, hid, xet, in_sem,
-                 s_x, s_r, s_g, s_row, s_dot, s_part, s_sum,
-                 v_x, v_r, v_g, v_row, v_dot, v_part, v_sum):
+                 rows_s, rows_r, dots_s, dots_r, part_s, part_r, mid_s, mid_r, sum_s, slope, hid, xet, in_sem,
+                 s_x, s_r, s_g, s_row, s_dot, s_part, s_mid, s_sum,
+                 v_x, v_r, v_g, v_row, v_dot, v_part, v_mid, v_sum):
     me = lax.axis_index('ep')
     tokens, hidden = x_ref.shape
     ff = w1.shape[1]
@@ -54,8 +54,6 @@
     plane = n // 4
     tokens_all = tokens * n
     numel = tokens_all * hidden
-    tile = 512
-    tiles = ff // tile
 
     low, high = lax.rem(me, plane), lax.div(me, plane)
     low_bits = [lax.rem(low, 2), lax.rem(lax.div(low, 2), 2), lax.div(low, 4)]
@@ -134,7 +132,8 @@
 
     fetched[3].wait()
     x = x_ref[...]
-    sx[...] = dot(disp, x).astype(BF16)
+    first_rows = plane * rows
+    sx[0:first_rows, :] = dot(disp[0:first_rows], x).astype(BF16)
 
     pl.semaphore_wait(barrier, n - 1)
 
@@ -161,6 +160,7 @@
         each_partner(pieces or quarters_of[c], lambda q, d: block(src, dst, send, recv, c, q, d).start())
 
     send_group(sx, xe, s_x, v_x, early)
+    sx[first_rows:, :] = dot(disp[first_rows:], x).astype(BF16)
     send_group(sx, xe, s_x, v_x, near)
     own_block(sx, xe, v_x)
     fetched[4].wait()
@@ -181,9 +181,20 @@
     g1 = jnp.sum(prob * hot1, axis=0, keepdims=True)
     g2 = jnp.sum(prob * hot2, axis=0, keepdims=True)
     gsum = g1 + g2
-    n1 = (g1 / gsum).astype(BF16).astype(F32)
-    n2 = (g2 / gsum).astype(BF16).astype(F32)
-    norm_rows = dot((hot1 * n1).astype(BF16), at1.astype(BF16), NT) + dot((hot2 * n2).astype(BF16), at2.astype(BF16), NT)
+    ratio1, ratio2 = g1 / gsum, g2 / gsum
+    n1 = ratio1.astype(BF16).astype(F32)
+    n2 = ratio2.astype(BF16).astype(F32)
+    mix = ratio1 * ratio2
+    exact = lax.Precision.HIGHEST
+    expert_f = expert_i.astype(F32)
+    e1f, e2f = jnp.sum(hot1 * expert_f, axis=0, keepdims=True), jnp.sum(hot2 * expert_f, axis=0, keepdims=True)
+
+    def placed(place, base):
+        return (place_i == jnp.where(place >= 0, place + base, -1)).astype(F32)
+
+    norm_rows = dot(hot1 * n1, at1, NT, precision=exact) + dot(hot2 * n2, at2, NT, precision=exact)
+    norm_rows = norm_rows + dot(hot1 * mix, placed(place1, 16), NT, precision=exact) + dot(hot2 * mix, placed(place2, 16), NT, precision=exact)
+    norm_rows = norm_rows + dot(hot1 * e2f, placed(place1, 104), NT, precision=exact) + dot(hot2 * e1f, placed(place2, 104), NT, precision=exact)
     sub_n, lane_n = iota((n, 128), 0), iota((n, 128), 1)
 
     def as_lanes(col, base):
@@ -211,8 +222,9 @@
     quarter = slot_row // rows // plane
     far = jnp.where(quarter == 0, order[0], jnp.where(quarter == 3, order[3], quarter - 1))
     source = (far * plane + slot_row // rows % plane) ^ me
-    pick = (source == iota((slots, n), 1)).astype(F32).astype(BF16)
-    mine = iota((slots, 128), 1) == iota((slots, 128), 0) % rows
+    pick = (source == iota((slots, n), 1)).astype(F32)
+    lane_s, row_s = iota((slots, 128), 1), iota((slots, 128), 0) % rows
+    mine = lane_s == row_s
     key1c, key2c = column(key1), column(key2)
     slot_l = iota((tokens, slots), 1)
     comb = ((slot_l == key1c) | (slot_l == key2c)).astype(F32).astype(BF16)
@@ -222,22 +234,13 @@
     def forward(c):
         at = group_at(c)
         settle(xe, v_x.at[c], at)
-        total_at = pl.ds(0, span[c][1])
-        acc[total_at, :] = jnp.zeros((span[c][1], hidden), F32)
-
-        @pl.loop(0, tiles)
-        def _(f):
-            cols = pl.ds(pl.multiple_of(f * tile, tile), tile)
-            pre = dot(xe[at, :], w1[:, cols])
-            sq = pre * pre
-            th = jnp.tanh(GELU_C * (pre + GELU_K * (sq * pre)))
-            cdf = 0.5 * (1.0 + th)
-            a = (pre * cdf).astype(BF16)
-            slope[at, cols] = cdf + (0.5 * GELU_C) * pre * (1.0 - th * th) * (1.0 + 3 * GELU_K * sq)
-            act[at, cols] = a
-            acc[total_at, :] += dot(a, w2[cols, :])
-
-        hid[at, :] = acc[total_at, :].astype(BF16)
+        pre = dot(xe[at, :], w1[...])
+        sq = pre * pre
+        th = jnp.tanh(GELU_C * (pre + GELU_K * (sq * pre)))
+        cdf = 0.5 * (1.0 + th)
+        slope[at, :] = cdf + (0.5 * GELU_C) * pre * (1.0 - th * th) * (1.0 + 3 * GELU_K * sq)
+        act[at, :] = (pre * cdf).astype(BF16)
+        hid[at, :] = dot(act[at, :], w2[...]).astype(BF16)
 
     def receive(c):
         at = group_at(c)
@@ -247,39 +250,20 @@
         norm = norms[start:start + size]
         gy[at, :] = (norm * rc).astype(BF16)
         d = jnp.sum(hid[at, :].astype(F32) * rc, axis=1, keepdims=True)
+        share = mixes[start:start + size] * d.astype(BF16).astype(F32) * signs[start:start + size]
+        part_s[...] += dot(share.astype(BF16), xe[at, :], TN)
         in_lane = jnp.where(mine[start:start + size], d, 0.0)
         dots_s[pl.ds(start // rows, size // rows), :] = jnp.sum(in_lane.reshape(size // rows, rows, 128), axis=1)
         return jnp.sum(norm * d, axis=0, keepdims=True)
 
     def backward(c):
         at = group_at(c)
-        total_at = pl.ds(0, span[c][1])
-        acc[total_at, :] = jnp.zeros((span[c][1], hidden), F32)
-
-        @pl.loop(0, tiles)
-        def _(f):
-            cols = pl.ds(pl.multiple_of(f * tile, tile), tile)
-            ga = dot(gy[at, :], w2[cols, :], NT).astype(BF16)
-            gp = (ga.astype(F32) * slope[at, cols]).astype(BF16)
-            gpre[at, cols] = gp
-            acc[total_at, :] += dot(gp, w1[:, cols], NT)
-
-        gs[at, :] = acc[total_at, :].astype(BF16)
+        ga = dot(gy[at, :], w2[...], NT).astype(BF16)
+        gpre[at, :] = (ga.astype(F32) * slope[at, :]).astype(BF16)
+        gs[at, :] = dot(gpre[at, :], w1[...], NT).astype(BF16)
 
     def send_back(c, pieces=None):
         send_group(gs, gback, s_g, v_g, c, pieces)
-
-    def grad_first(lo, hi):
-        @pl.loop(lo, hi)
-        def _(f):
-            cols = pl.ds(pl.multiple_of(f * tile, tile), tile)
-            gw1[:, cols] = dot(xet[...], gpre[:, cols]).astype(BF16)
-
-    def grad_second(lo, hi):
-        @pl.loop(lo, hi)
-        def _(f):
-            cols = pl.ds(pl.multiple_of(f * tile, tile), tile)
-            gw2[cols, :] = dot(act[:, cols], gy[...], TN).astype(BF16)
 
     forward(early)
     forward(near)
@@ -288,7 +272,15 @@
     total = jnp.sum(all_rows, axis=0, keepdims=True)
     frac = as_column(total, 32) / tokens_all
     mean_prob = as_column(total, 64) / tokens_all
-    norms = jnp.sum(jnp.where(mine, dot(pick, all_rows.astype(BF16)), 0.0), axis=1, keepdims=True)
+    wide = dot(pick, all_rows, precision=exact)
+    norms = jnp.sum(jnp.where(mine, wide, 0.0), axis=1, keepdims=True)
+    mixes = jnp.sum(jnp.where(lane_s == row_s + 16, wide, 0.0), axis=1, keepdims=True)
+    others = jnp.sum(jnp.where(lane_s == row_s + 104, wide, 0.0), axis=1, keepdims=True)
+    column_i = iota((slots, n), 1)
+    signs = (column_i == me).astype(F32) - (column_i.astype(F32) == others).astype(F32)
+    aux_prob = (ALPHA * hidden * n) * frac
+    aux_log = prob * (aux_prob - jnp.sum(prob * aux_prob, axis=0, keepdims=True))
+    part_s[...] = dot(aux_log.astype(BF16), x_ref[...])
 
     loss_part = receive(early)
     backward(early)
@@ -302,44 +294,74 @@
     xet[...] = jnp.transpose(xe[...])
     loss_part = loss_part + receive(late)
     dots_s[...] = dots_s[...] + jnp.where(lane_1 == 16, loss_part, 0.0)
+
+    share_rows = n // plane
+
+    def line_copy(src, src_row, dst, dst_row, send, recv, q, d):
+        return pltpu.make_async_remote_copy(src.at[pl.ds(src_row, 1)], dst.at[pl.ds(dst_row, 1)], send.at[q], recv.at[0], device_id=(d,), device_id_type=MESH)
+
+    def own_line(src, src_row, dst, dst_row, recv):
+        pltpu.make_async_copy(src.at[pl.ds(src_row, 1)], dst.at[pl.ds(dst_row, 1)], recv.at[0]).start()
+
+    def plane_peers(body):
+        @pl.loop(1, plane)
+        def _(step):
+            d = partner(1, step)
+            for j in range(share_rows):
+                body(step * share_rows + j, d, lax.rem(d, plane) * share_rows + j, low * share_rows + j, j)
+
+    def scatter(q, d, theirs, ours, j):
+        return line_copy(part_s, theirs, part_r, ours, s_part, v_part, q, d)
+
+    def line_peers(body):
+        for quarter in (0, 3, 2):
+            d = partner(quarter, 0)
+            for j in range(share_rows):
+                body(quarter * share_rows + j, d, j)
+
+    def exchange(q, d, j):
+        return line_copy(mid_s, j, mid_r, high * share_rows + j, s_mid, v_mid, q, d)
+
+    def gather(q, d, theirs, ours, j):
+        return line_copy(sum_s, j, gg_ref, ours, s_sum, v_sum, q, d)
+
+    plane_peers(lambda *a: scatter(*a).start())
+    for j in range(share_rows):
+        own_line(part_s, low * share_rows + j, part_r, low * share_rows + j, v_part)
     each_partner(everyone, lambda q, d: one_row(dots_s, dots_r, q, s_dot, v_dot, q, d).start())
     own_row(dots_s, dots_r, plane, v_dot)
     send_back(early, ((0, split_early, plane),))
     backward(late)
     send_back(late, ((3, 0, split_late),))
-    grad_first(0, 2)
+    gw1[...] = dot(xet[...], gpre[...]).astype(BF16)
+
+    settle(part_r, v_part.at[0], pl.ds(0, n))
+    fold = part_r[0:8, :] + part_r[8:16, :] + part_r[16:24, :] + part_r[24:32, :]
+    mid_s[0:4, :] = fold[0:4] + fold[4:8]
+    line_peers(lambda *a: exchange(*a).start())
+    for j in range(share_rows):
+        own_line(mid_s, j, mid_r, high * share_rows + j, v_mid)
+    send_back(late, ((3, split_late, plane),))
+    gw2[...] = dot(act[...], gy[...], TN).astype(BF16)
+
+    settle(mid_r, v_mid.at[0], pl.ds(0, 16))
+    fold = mid_r[0:8, :] + mid_r[8:16, :]
+    sum_s[0:4, :] = fold[0:4] + fold[4:8]
+    plane_peers(lambda *a: gather(*a).start())
+    for j in range(share_rows):
+        own_line(sum_s, j, gg_ref, low * share_rows + j, v_sum)
 
     settle(dots_r, v_dot.at[0], pl.ds(0, n))
     all_dots = dots_r[...]
-    exact = lax.Precision.HIGHEST
     d1 = jnp.sum(dot(all_dots, hot1, TN, precision=exact) * at1, axis=0, keepdims=True)
     d2 = jnp.sum(dot(all_dots, hot2, TN, precision=exact) * at2, axis=0, keepdims=True)
-    d1 = d1.astype(BF16).astype(F32)
-    d2 = d2.astype(BF16).astype(F32)
-    gate_sq = gsum * gsum
-    up1 = (d1 - d2) * g2 / gate_sq
-    up2 = (d2 - d1) * g1 / gate_sq
-    gprob = up1 * hot1 + up2 * hot2 + (ALPHA * hidden * n) * frac
-    glog = (prob * (gprob - jnp.sum(prob * gprob, axis=0, keepdims=True))).astype(BF16)
-    part_s[...] = dot(glog, x_ref[...])
-    each_partner(everyone, lambda q, d: one_row(part_s, part_r, d, s_part, v_part, q, d).start())
-    own_row(part_s, part_r, me, v_part)
-    send_back(late, ((3, split_late, plane),))
-    grad_first(2, tiles)
+    apart = d1.astype(BF16).astype(F32) - d2.astype(BF16).astype(F32)
+    glog = (aux_log + (mix * apart) * (hot1 - hot2)).astype(BF16)
 
     both = jnp.sum(jnp.where(lane_1 == 96, total, 0.0), axis=1, keepdims=True)
     both = both + jnp.sum(jnp.where(lane_1 == 16, jnp.sum(all_dots, axis=0, keepdims=True), 0.0), axis=1, keepdims=True)
     aux = jnp.sum(frac * mean_prob, axis=0, keepdims=True) * n
     loss_ref[...] = jnp.broadcast_to(both / numel + ALPHA * aux, loss_ref.shape)
-    grad_second(0, 2)
-
-    settle(part_r, v_part.at[0], pl.ds(0, n))
-    sum_s[0:1, :] = jnp.sum(part_r[...], axis=0, keepdims=True)
-    each_partner(everyone, lambda q, d: one_row(sum_s, gg_ref, 0, s_sum, v_sum, q, d).start())
-    own_row(sum_s, gg_ref, 0, v_sum)
-
-    grad_second(2, tiles)
-
     out = r_ref[...].astype(F32) + dot(glog, wg_ref[...], TN)
     for c in (near, early, late):
         start, size = span[c]
@@ -350,8 +372,9 @@
     settle(gg_ref, v_sum.at[0], pl.ds(0, n))
     each_partner(everyone, lambda q, d: one_row(rows_s, rows_r, d, s_row, v_row, q, d).wait_send())
     each_partner(everyone, lambda q, d: one_row(dots_s, dots_r, q, s_dot, v_dot, q, d).wait_send())
-    each_partner(everyone, lambda q, d: one_row(part_s, part_r, d, s_part, v_part, q, d).wait_send())
-    each_partner(everyone, lambda q, d: one_row(sum_s, gg_ref, 0, s_sum, v_sum, q, d).wait_send())
+    plane_peers(lambda *a: scatter(*a).wait_send())
+    line_peers(lambda *a: exchange(*a).wait_send())
+    plane_peers(lambda *a: gather(*a).wait_send())
     for ref, sem in ((sx, s_x), (sr, s_r), (gs, s_g)):
         settle(ref, sem.at[early], group_at(early))
         settle(ref, sem.at[near], pl.ds(own + rows, span[near][1] - rows))
@@ -407,13 +430,14 @@
                 pltpu.VMEM((n, hidden), F32),
                 pltpu.VMEM((n, hidden), F32),
                 pltpu.VMEM((8, hidden), F32),
-                pltpu.VMEM((slots // 2, hidden), F32),
+                pltpu.VMEM((16, hidden), F32),
+                pltpu.VMEM((8, hidden), F32),
                 pltpu.VMEM((slots, ff), F32),
                 pltpu.VMEM((slots, hidden), BF16),
                 pltpu.VMEM((hidden, slots), BF16),
                 dma((8,)),
-                dma((3,)), dma((3,)), dma((3,)), dma((n,)), dma((n,)), dma((n,)), dma((n,)),
-                dma((3,)), dma((3,)), dma((3,)), dma((1,)), dma((1,)), dma((1,)), dma((1,)),
+                dma((3,)), dma((3,)), dma((3,)), dma((n,)), dma((n,)), dma((n,)), dma((16,)), dma((n,)),
+                dma((3,)), dma((3,)), dma((3,)), dma((1,)), dma((1,)), dma((1,)), dma((1,)), dma((1,)),
             ],
             compiler_params=pltpu.CompilerParams(collective_id=0, has_side_effects=True, vmem_limit_bytes=44 * 1024 * 1024),
         )(*(pltpu.with_memory_space_constraint(a, pltpu.HBM) for a in (

time: 77.6 us -> 74.4 us (0.959)
  Pallas kernels: 76.8 us -> 73.4 us
    pallas_call x1, Pallas kernels: 72.5 us -> 69.1 us  [layer_body(): pl.pallas_call(functools.partial(layer_kernel, n, cap, seq), name='moe_la...]
where the time goes in v5:
time: 74.4 us; the launch traced here: 74.2 us
  Pallas kernels  73.4 us (99%)
  between operations  0.82 us (1%)
    pallas_call x1, Pallas kernels, layer_body(): pl.pallas_call(functools.partial(layer_kernel, n, cap, seq), name='moe_la...  69.1 us
    pallas_call x1, Pallas kernels, layer_body(): pl.pallas_call(write_kernel, name='write_results', out_shape=(jax.ShapeDt...  4.3 us

profile of v5, /device:TPU:0, one launch (start us, length us, event | category | flops | bytes accessed | tf_op | source)
XLA Modules:
  0.0 74.2 jit_solution(1074808388941581893)
XLA Ops:
  0.6 69.1 %moe_layer.1 = (f32[8,128]{1,0:T(8,128)S(1)}, bf16[256,768]{1,0:T(8,128)(2,1)S(1)}, f32[32,768]{1,0:T(8,128)S(1)}, bf16[768,3072]{1,0:T(8,128)(2,1)S(1)}, bf16[3072,768]{1,0:T(8,128)(2,1)S(1)}) custom-call(s32[4,64]{1,0:T(4,128)} %e1_hbm.1, s32[4,64]{1,0:T(4,128)} %e2_hbm.1, s32[4,64]{1,0:T(4,128)} %k2_hbm.1, bf16[256,768]{1,0:T(8,128)(2,1)} %bitcast.12, ...), custom_call_target="tpu_custom_call" | custom-call | tf_op jit(solution)/shard_map/moe_layer/pallas_call | solution.py:396
  69.7 4.3 %write_results.1 = (f32[1,1]{1,0:T(1,128)}, bf16[256,768]{1,0:T(8,128)(2,1)}, f32[32,768]{1,0:T(8,128)}, bf16[768,3072]{1,0:T(8,128)(2,1)}, bf16[3072,768]{1,0:T(8,128)(2,1)}) custom-call(f32[8,128]{1,0:T(8,128)S(1)} %get-tuple-element.15.loss_v, bf16[256,768]{1,0:T(8,128)(2,1)S(1)} %get-tuple-element.16.gx_v, f32[32,768]{1,0:T(8,128)S(1)} %get-tuple-element.17.gg_v, ...), custom_call_target="tpu_custom_call" | custom-call | tf_op jit(solution)/shard_map/write_results/pallas_call | solution.py:445

commit v6 on v5

--- a/solution.py
+++ b/solution.py
@@ -284,8 +284,8 @@
 
     loss_part = receive(early)
     backward(early)
-    split_early, split_late = 5, 2
-    send_back(early, ((0, 0, split_early),))
+    split_late = 1
+    send_back(early)
     loss_part = loss_part + receive(near)
     backward(near)
     send_back(near)
@@ -330,11 +330,8 @@
         own_line(part_s, low * share_rows + j, part_r, low * share_rows + j, v_part)
     each_partner(everyone, lambda q, d: one_row(dots_s, dots_r, q, s_dot, v_dot, q, d).start())
     own_row(dots_s, dots_r, plane, v_dot)
-    send_back(early, ((0, split_early, plane),))
     backward(late)
     send_back(late, ((3, 0, split_late),))
-    gw1[...] = dot(xet[...], gpre[...]).astype(BF16)
-
     settle(part_r, v_part.at[0], pl.ds(0, n))
     fold = part_r[0:8, :] + part_r[8:16, :] + part_r[16:24, :] + part_r[24:32, :]
     mid_s[0:4, :] = fold[0:4] + fold[4:8]
@@ -342,6 +339,7 @@
     for j in range(share_rows):
         own_line(mid_s, j, mid_r, high * share_rows + j, v_mid)
     send_back(late, ((3, split_late, plane),))
+    gw1[...] = dot(xet[...], gpre[...]).astype(BF16)
     gw2[...] = dot(act[...], gy[...], TN).astype(BF16)
 
     settle(mid_r, v_mid.at[0], pl.ds(0, 16))
@@ -363,22 +361,29 @@
     aux = jnp.sum(frac * mean_prob, axis=0, keepdims=True) * n
     loss_ref[...] = jnp.broadcast_to(both / numel + ALPHA * aux, loss_ref.shape)
     out = r_ref[...].astype(F32) + dot(glog, wg_ref[...], TN)
-    for c in (near, early, late):
-        start, size = span[c]
-        settle(gback, v_g.at[c], group_at(c))
-        out = out + dot(comb[:, start:start + size], gback[group_at(c), :])
-    gx_ref[...] = out.astype(BF16)
-
-    settle(gg_ref, v_sum.at[0], pl.ds(0, n))
     each_partner(everyone, lambda q, d: one_row(rows_s, rows_r, d, s_row, v_row, q, d).wait_send())
     each_partner(everyone, lambda q, d: one_row(dots_s, dots_r, q, s_dot, v_dot, q, d).wait_send())
     plane_peers(lambda *a: scatter(*a).wait_send())
     line_peers(lambda *a: exchange(*a).wait_send())
+
+    def sent(ref, sem, groups_sent):
+        for c in groups_sent:
+            start, size = span[c]
+            settle(ref, sem.at[c], pl.ds(own + rows, size - rows) if c == near else pl.ds(start, size))
+
+    sent(sx, s_x, (early, near, late))
+    sent(sr, s_r, (early, near, late))
+    sent(gs, s_g, (early, near))
+    for c in (near, early):
+        start, size = span[c]
+        settle(gback, v_g.at[c], group_at(c))
+        out = out + dot(comb[:, start:start + size], gback[group_at(c), :])
     plane_peers(lambda *a: gather(*a).wait_send())
-    for ref, sem in ((sx, s_x), (sr, s_r), (gs, s_g)):
-        settle(ref, sem.at[early], group_at(early))
-        settle(ref, sem.at[near], pl.ds(own + rows, span[near][1] - rows))
-        settle(ref, sem.at[late], group_at(late))
+    settle(gg_ref, v_sum.at[0], pl.ds(0, n))
+    sent(gs, s_g, (late,))
+    start, size = span[late]
+    settle(gback, v_g.at[late], group_at(late))
+    gx_ref[...] = (out + dot(comb[:, start:start + size], gback[group_at(late), :])).astype(BF16)
 
 
 def solution(mesh):

time: 74.4 us -> 72 us (0.968)
  Pallas kernels: 73.4 us -> 71 us
    pallas_call x1, Pallas kernels: 69.1 us -> 66.7 us  [layer_body(): pl.pallas_call(functools.partial(layer_kernel, n, cap, seq), name='moe_la...]
where the time goes in v6:
time: 72 us; the launch traced here: 71.8 us
  Pallas kernels  71 us (99%)
  between operations  0.8 us (1%)
    pallas_call x1, Pallas kernels, layer_body(): pl.pallas_call(functools.partial(layer_kernel, n, cap, seq), name='moe_la...  66.7 us
    pallas_call x1, Pallas kernels, layer_body(): pl.pallas_call(write_kernel, name='write_results', out_shape=(jax.ShapeDt...  4.3 us

profile of v6, /device:TPU:0, one launch (start us, length us, event | category | flops | bytes accessed | tf_op | source)
XLA Modules:
  0.0 71.8 jit_solution(17145925106962522478)
XLA Ops:
  0.6 66.7 %moe_layer.1 = (f32[8,128]{1,0:T(8,128)S(1)}, bf16[256,768]{1,0:T(8,128)(2,1)S(1)}, f32[32,768]{1,0:T(8,128)S(1)}, bf16[768,3072]{1,0:T(8,128)(2,1)S(1)}, bf16[3072,768]{1,0:T(8,128)(2,1)S(1)}) custom-call(s32[4,64]{1,0:T(4,128)} %e1_hbm.1, s32[4,64]{1,0:T(4,128)} %e2_hbm.1, s32[4,64]{1,0:T(4,128)} %k2_hbm.1, bf16[256,768]{1,0:T(8,128)(2,1)} %bitcast.12, ...), custom_call_target="tpu_custom_call" | custom-call | tf_op jit(solution)/shard_map/moe_layer/pallas_call | solution.py:401
  67.4 4.3 %write_results.1 = (f32[1,1]{1,0:T(1,128)}, bf16[256,768]{1,0:T(8,128)(2,1)}, f32[32,768]{1,0:T(8,128)}, bf16[768,3072]{1,0:T(8,128)(2,1)}, bf16[3072,768]{1,0:T(8,128)(2,1)}) custom-call(f32[8,128]{1,0:T(8,128)S(1)} %get-tuple-element.15.loss_v, bf16[256,768]{1,0:T(8,128)(2,1)S(1)} %get-tuple-element.16.gx_v, f32[32,768]{1,0:T(8,128)S(1)} %get-tuple-element.17.gg_v, ...), custom_call_target="tpu_custom_call" | custom-call | tf_op jit(solution)/shard_map/write_results/pallas_call | solution.py:450

commit v7 on v6

--- a/solution.py
+++ b/solution.py
@@ -73,7 +73,8 @@
             first = max(lo, 1) if order[quarter] == 0 else lo
 
             @pl.loop(first, hi)
-            def _(step):
+            def _(count):
+                step = hi - 1 + first - count
                 body(quarter * plane + step, partner(quarter, step))
 
     everyone = tuple((quarter, 0, plane) for quarter in (0, 3, 1, 2))
@@ -328,17 +329,17 @@
     plane_peers(lambda *a: scatter(*a).start())
     for j in range(share_rows):
         own_line(part_s, low * share_rows + j, part_r, low * share_rows + j, v_part)
-    each_partner(everyone, lambda q, d: one_row(dots_s, dots_r, q, s_dot, v_dot, q, d).start())
-    own_row(dots_s, dots_r, plane, v_dot)
     backward(late)
-    send_back(late, ((3, 0, split_late),))
+    send_back(late, ((3, plane - split_late, plane),))
     settle(part_r, v_part.at[0], pl.ds(0, n))
     fold = part_r[0:8, :] + part_r[8:16, :] + part_r[16:24, :] + part_r[24:32, :]
     mid_s[0:4, :] = fold[0:4] + fold[4:8]
     line_peers(lambda *a: exchange(*a).start())
     for j in range(share_rows):
         own_line(mid_s, j, mid_r, high * share_rows + j, v_mid)
-    send_back(late, ((3, split_late, plane),))
+    each_partner(everyone, lambda q, d: one_row(dots_s, dots_r, q, s_dot, v_dot, q, d).start())
+    own_row(dots_s, dots_r, plane, v_dot)
+    send_back(late, ((3, 0, plane - split_late),))
     gw1[...] = dot(xet[...], gpre[...]).astype(BF16)
     gw2[...] = dot(act[...], gy[...], TN).astype(BF16)
 

time: 72 us -> 69.6 us (0.967)
  Pallas kernels: 71 us -> 68.6 us
    pallas_call x1, Pallas kernels: 66.7 us -> 64.3 us  [layer_body(): pl.pallas_call(functools.partial(layer_kernel, n, cap, seq), name='moe_la...]
where the time goes in v7:
time: 69.6 us; the launch traced here: 69.4 us
  Pallas kernels  68.6 us (99%)
  between operations  0.8 us (1%)
    pallas_call x1, Pallas kernels, layer_body(): pl.pallas_call(functools.partial(layer_kernel, n, cap, seq), name='moe_la...  64.3 us
    pallas_call x1, Pallas kernels, layer_body(): pl.pallas_call(write_kernel, name='write_results', out_shape=(jax.ShapeDt...  4.3 us

profile of v7, /device:TPU:0, one launch (start us, length us, event | category | flops | bytes accessed | tf_op | source)
XLA Modules:
  0.0 69.4 jit_solution(7092342355785308019)
XLA Ops:
  0.6 64.3 %moe_layer.1 = (f32[8,128]{1,0:T(8,128)S(1)}, bf16[256,768]{1,0:T(8,128)(2,1)S(1)}, f32[32,768]{1,0:T(8,128)S(1)}, bf16[768,3072]{1,0:T(8,128)(2,1)S(1)}, bf16[3072,768]{1,0:T(8,128)(2,1)S(1)}) custom-call(s32[4,64]{1,0:T(4,128)} %e1_hbm.1, s32[4,64]{1,0:T(4,128)} %e2_hbm.1, s32[4,64]{1,0:T(4,128)} %k2_hbm.1, bf16[256,768]{1,0:T(8,128)(2,1)} %bitcast.12, ...), custom_call_target="tpu_custom_call" | custom-call | tf_op jit(solution)/shard_map/moe_layer/pallas_call | solution.py:402
  65.0 4.3 %write_results.1 = (f32[1,1]{1,0:T(1,128)}, bf16[256,768]{1,0:T(8,128)(2,1)}, f32[32,768]{1,0:T(8,128)}, bf16[768,3072]{1,0:T(8,128)(2,1)}, bf16[3072,768]{1,0:T(8,128)(2,1)}) custom-call(f32[8,128]{1,0:T(8,128)S(1)} %get-tuple-element.15.loss_v, bf16[256,768]{1,0:T(8,128)(2,1)S(1)} %get-tuple-element.16.gx_v, f32[32,768]{1,0:T(8,128)S(1)} %get-tuple-element.17.gg_v, ...), custom_call_target="tpu_custom_call" | custom-call | tf_op jit(solution)/shard_map/write_results/pallas_call | solution.py:451

commit v8 on v7

--- a/solution.py
+++ b/solution.py
@@ -285,7 +285,6 @@
 
     loss_part = receive(early)
     backward(early)
-    split_late = 1
     send_back(early)
     loss_part = loss_part + receive(near)
     backward(near)
@@ -330,7 +329,6 @@
     for j in range(share_rows):
         own_line(part_s, low * share_rows + j, part_r, low * share_rows + j, v_part)
     backward(late)
-    send_back(late, ((3, plane - split_late, plane),))
     settle(part_r, v_part.at[0], pl.ds(0, n))
     fold = part_r[0:8, :] + part_r[8:16, :] + part_r[16:24, :] + part_r[24:32, :]
     mid_s[0:4, :] = fold[0:4] + fold[4:8]
@@ -339,7 +337,7 @@
         own_line(mid_s, j, mid_r, high * share_rows + j, v_mid)
     each_partner(everyone, lambda q, d: one_row(dots_s, dots_r, q, s_dot, v_dot, q, d).start())
     own_row(dots_s, dots_r, plane, v_dot)
-    send_back(late, ((3, 0, plane - split_late),))
+    send_back(late, ((3, 0, plane),))
     gw1[...] = dot(xet[...], gpre[...]).astype(BF16)
     gw2[...] = dot(act[...], gy[...], TN).astype(BF16)
 

time: 69.6 us -> 69.3 us (level)
  no operation moved by 1% of the time
where the time goes in v8:
time: 69.3 us; the launch traced here: 69.1 us
  Pallas kernels  68.3 us (99%)
  between operations  0.8 us (1%)
    pallas_call x1, Pallas kernels, layer_body(): pl.pallas_call(functools.partial(layer_kernel, n, cap, seq), name='moe_la...  64 us
    pallas_call x1, Pallas kernels, layer_body(): pl.pallas_call(write_kernel, name='write_results', out_shape=(jax.ShapeDt...  4.3 us

profile of v8, /device:TPU:0, one launch (start us, length us, event | category | flops | bytes accessed | tf_op | source)
XLA Modules:
  0.0 69.1 jit_solution(10168370623427965085)
XLA Ops:
  0.6 64.0 %moe_layer.1 = (f32[8,128]{1,0:T(8,128)S(1)}, bf16[256,768]{1,0:T(8,128)(2,1)S(1)}, f32[32,768]{1,0:T(8,128)S(1)}, bf16[768,3072]{1,0:T(8,128)(2,1)S(1)}, bf16[3072,768]{1,0:T(8,128)(2,1)S(1)}) custom-call(s32[4,64]{1,0:T(4,128)} %e1_hbm.1, s32[4,64]{1,0:T(4,128)} %e2_hbm.1, s32[4,64]{1,0:T(4,128)} %k2_hbm.1, bf16[256,768]{1,0:T(8,128)(2,1)} %bitcast.12, ...), custom_call_target="tpu_custom_call" | custom-call | tf_op jit(solution)/shard_map/moe_layer/pallas_call | solution.py:400
  64.7 4.3 %write_results.1 = (f32[1,1]{1,0:T(1,128)}, bf16[256,768]{1,0:T(8,128)(2,1)}, f32[32,768]{1,0:T(8,128)}, bf16[768,3072]{1,0:T(8,128)(2,1)}, bf16[3072,768]{1,0:T(8,128)(2,1)}) custom-call(f32[8,128]{1,0:T(8,128)S(1)} %get-tuple-element.15.loss_v, bf16[256,768]{1,0:T(8,128)(2,1)S(1)} %get-tuple-element.16.gx_v, f32[32,768]{1,0:T(8,128)S(1)} %get-tuple-element.17.gg_v, ...), custom_call_target="tpu_custom_call" | custom-call | tf_op jit(solution)/shard_map/write_results/pallas_call | solution.py:449
